TPU v7x, 32 devices: a whole 2x2x4 slice. The times are simulated.
32 devices in a mesh: outer: 2 (over core), dp: 4 (over z), tensor: 4 (over y, x).
Axes of the slice: x: 2, y: 2, z: 4, core: 2. Of those that a mesh axis runs over, the one named last changes fastest.
Arguments:
- attn: bfloat16 [2048, 8192], P(('outer', 'dp'), 'tensor'), may hold values from -6 to 6
- out_weight: bfloat16 [8192, 8192], P(None, 'tensor'), may hold values from -0.0625 to 0.0625
- resid: bfloat16 [2048, 8192], P(('outer', 'dp'), 'tensor'), may hold values from -8 to 8
- norm_gain: bfloat16 [8192], P('tensor'), may hold values from 0.5 to 1.5
- head: bfloat16 [8192], P('tensor'), may hold values from -1 to 1
- lengths: int32 [32], P(('outer', 'dp')), may hold values from 1 to 64
- pairs: int32 [32, 2], P(('outer', 'dp')), may hold values from 0 to 3, as said below
- pair_valid: int32 [32], P(('outer', 'dp')), may hold values from 0 to 1, as said below
- loss_scale: float32 [1], replicated, may hold values from 1024 to 8192
Outputs:
- loss: float32 [1], replicated
- grad_out_proj: float32 [8192, 8192], P(('outer', 'dp'), 'tensor')
- grad_gain: float32 [8192], P('tensor')
- grad_head: float32 [8192], P('tensor')
Inputs may be any that keep to these rules, and one draw needn't show every extreme that they name: `pairs`: in each pair the two numbers differ; the first pair of each replica is valid. `pair_valid`: the first of each replica's 4 entries is 1.
All inputs are finite; a program needn't handle non-finite values.
Results may differ from a plain program's by a relative error of at most 0.003.
Values may be sent and summed in bfloat16 or wider, within the bound.
A program may use at most 128 MiB of HBM per device.

v0:
```python
import functools

import jax
import jax.numpy as jnp
from jax import lax
from jax.experimental import pallas as pl
from jax.experimental.pallas import tpu as pltpu
from jax.sharding import PartitionSpec as P

MESH = pl.DeviceIdType.MESH
F32 = jnp.float32
BF16 = jnp.bfloat16
SLOTS = 3


def bits_of(count):
    return count.bit_length() - 1


def flip(index, mask, bits):
    out = 0
    for j in range(bits):
        out = out + ((index // 2**j + mask // 2**j) % 2) * 2**j
    return out


def kernel(
    sizes,
    attn,
    weight,
    resid,
    both,
    pool,
    select,
    scaled_valid,
    valid,
    vsum,
    grad,
    qtot,
    ltot,
    ctot,
    exch,
    attn_all,
    acc,
    wbuf,
    attn_t,
    part,
    got,
    z,
    dp,
    stat,
    stat_in,
    cin,
    lsrc,
    lin,
    qsrc,
    qin,
    wsem,
    rs_send,
    rs_recv,
    st_send,
    st_recv,
    c_send,
    c_recv,
    l_send,
    l_recv,
    q_send,
    q_recv,
    ag_local,
    ag_right,
    ag_left,
    ag_out,
    ag_recv,
    z_send,
    b_send,
    e_recv,
    o_sem,
):
    T, O, Z = sizes
    N = O * Z
    bits = bits_of(T)
    R = N // T
    tok, feats = resid.shape
    width = feats * T
    blk = width // N
    tile = wbuf.shape[1]
    per = feats // tile
    o, p, t = lax.axis_index("outer"), lax.axis_index("dp"), lax.axis_index("tensor")
    me = o * Z + p

    def replica(k):
        return (k // Z, k % Z, t)

    def tensor_peer(r):
        return (o, p, flip(t, r, bits))

    barrier = pltpu.get_barrier_semaphore()
    for r in range(1, T):
        pl.semaphore_signal(barrier, inc=1, device_id=tensor_peer(r), device_id_type=MESH)
    for d in range(1, N):
        pl.semaphore_signal(barrier, inc=1, device_id=replica((me + d) % N), device_id_type=MESH)

    def load(i):
        target = flip(t, T - 1 - i // per, bits)
        start = pl.multiple_of(target * feats + (i % per) * tile, tile)
        return pltpu.make_async_copy(
            weight.at[pl.ds(start, tile)], wbuf.at[i % SLOTS], wsem.at[i % SLOTS]
        )

    for i in range(min(SLOTS - 1, T * per)):
        load(i).start()

    def turn_attn(c, carry):
        cols = pl.ds(pl.multiple_of(c * 128, 128), 128)
        attn_t[cols, :] = attn[:, cols].astype(F32).T.astype(BF16)
        return carry

    lax.fori_loop(0, feats // 128, turn_attn, 0)
    pl.semaphore_wait(barrier, T - 1 + N - 1)

    def peer_copy(src, dst, send, recv, d):
        return pltpu.make_async_remote_copy(
            src_ref=src,
            dst_ref=dst.at[d],
            send_sem=send.at[d],
            recv_sem=recv.at[d],
            device_id=replica((me + d) % N),
            device_id_type=MESH,
        )

    def block_rows(outer, b):
        return outer * Z + b

    def ag_copy(src, b, send, where):
        return pltpu.make_async_remote_copy(
            src_ref=src,
            dst_ref=attn_all.at[block_rows(o, b)],
            send_sem=send,
            recv_sem=ag_recv.at[o, b],
            device_id=where,
            device_id_type=MESH,
        )

    def right_copy(s):
        b = (p + Z - s) % Z
        src = attn if s == 0 else attn_all.at[block_rows(o, b)]
        return ag_copy(src, b, ag_right.at[s], (o, (p + 1) % Z, t))

    def left_copy(s):
        b = (p + s) % Z
        src = attn if s == 0 else attn_all.at[block_rows(o, b)]
        return ag_copy(src, b, ag_left.at[s], (o, (p + Z - 1) % Z, t))

    def right_sends(s):
        return (p >= s) & (p < Z - 1)

    def left_sends(s):
        return (p + s < Z) & (p > 0)

    def out_copy(b, e, own=False):
        src = attn if own else attn_all.at[block_rows(o, b)]
        return ag_copy(src, b, ag_out.at[e, b], ((o + e) % O, p, t))

    def arrived(outer, b):
        rows = attn_all.at[block_rows(outer, b)]
        return pltpu.make_async_remote_copy(
            src_ref=rows,
            dst_ref=rows,
            send_sem=ag_out.at[0, 0],
            recv_sem=ag_recv.at[outer, b],
            device_id=(o, (p + 1) % Z, t),
            device_id_type=MESH,
        )

    def arrival(s):
        for ok, b in ((p - 1 - s >= 0, (p + Z - 1 - s) % Z), (p + 1 + s < Z, (p + 1 + s) % Z)):

            @pl.when(ok)
            def _():
                arrived(o, b).wait_recv()
                for e in range(1, O):
                    out_copy(b, e).start()

        if s + 1 < Z - 1:
            for ok, copy in ((right_sends(s + 1), right_copy), (left_sends(s + 1), left_copy)):

                @pl.when(ok)
                def _():
                    copy(s + 1).start()

    for ok, copy in ((right_sends(0), right_copy), (left_sends(0), left_copy)):

        @pl.when(ok)
        def _():
            copy(0).start()

    for e in range(1, O):
        out_copy(p, e, True).start()
    own_rows = pltpu.make_async_copy(attn, attn_all.at[block_rows(o, p)], ag_local)
    own_rows.start()
    for d in range(1, N):
        peer_copy(vsum, cin, c_send, c_recv, d).start()

    def rs_copy(r, j):
        return pltpu.make_async_remote_copy(
            src_ref=part.at[r, j],
            dst_ref=got.at[r, j],
            send_sem=rs_send.at[r, j],
            recv_sem=rs_recv.at[r, j],
            device_id=tensor_peer(r),
            device_id_type=MESH,
        )

    def project(i, carry):
        @pl.when(i + SLOTS - 1 < T * per)
        def _():
            load(i + SLOTS - 1).start()

        load(i).wait()
        r, j = T - 1 - i // per, i % per
        part[r, j] = jnp.dot(
            wbuf[i % SLOTS], attn_t[...], preferred_element_type=F32
        ).astype(BF16)

        @pl.when(r > 0)
        def _():
            rs_copy(r, j).start()

        return carry

    lax.fori_loop(0, T * per, project, 0)

    def rows_of(j):
        return pl.ds(pl.multiple_of(j * tile, tile), tile)

    def turn_resid(j, carry):
        z[rows_of(j), :] = resid[:, rows_of(j)].astype(F32).T + part[0, j].astype(F32)
        return carry

    lax.fori_loop(0, per, turn_resid, 0)

    def clear(j, carry):
        acc[pl.ds(pl.multiple_of(j * 128, 128), 128), :] = jnp.zeros((128, acc.shape[1]), F32)
        return carry

    lax.fori_loop(0, blk // 128, clear, 0)
    arrival(0)

    def gather_z(j, carry):
        squares, heads = carry
        total = z[rows_of(j), :]
        for r in range(T - 1, 0, -1):
            rs_copy(r, j).wait_recv()
            total = total + got[r, j].astype(F32)
        z[rows_of(j), :] = total
        squares = squares + jnp.sum(total * total, axis=0, keepdims=True)
        heads = heads + jnp.sum(total * both[rows_of(j), :], axis=0, keepdims=True)
        return squares, heads

    zero = jnp.zeros((1, tok), F32)
    squares, heads = lax.fori_loop(0, per, gather_z, (zero, zero))
    stat[0:1, :] = squares
    stat[1:2, :] = heads

    def stat_copy(r):
        return pltpu.make_async_remote_copy(
            src_ref=stat,
            dst_ref=stat_in.at[r],
            send_sem=st_send.at[r],
            recv_sem=st_recv.at[r],
            device_id=tensor_peer(r),
            device_id_type=MESH,
        )

    for r in range(1, T):
        stat_copy(r).start()
    count = vsum[0:1, 0:1]
    for d in range(1, N):
        peer_copy(vsum, cin, c_send, c_recv, d).wait_recv()
        count = count + cin[d, 0:1, 0:1]
    if Z > 2:
        arrival(1)
    for r in range(1, T):
        stat_copy(r).wait_recv()
        squares = squares + stat_in[r, 0:1, :]
        heads = heads + stat_in[r, 1:2, :]
    inv = 1.0 / jnp.sqrt(squares / width + 1e-05)
    score = heads * inv
    reward = jnp.sum(pool[...] * score, axis=1, keepdims=True)
    margin = jnp.sum(select[...] * reward, axis=0, keepdims=True)
    soft = jnp.maximum(-margin, 0.0) + jnp.log1p(jnp.exp(-jnp.abs(margin)))
    loss = jnp.sum(valid[...] * soft, axis=1, keepdims=True)
    dmargin = scaled_valid[...] * jax.nn.sigmoid(-margin) / count
    dreward = jnp.sum(select[...] * dmargin, axis=1, keepdims=True)
    dscore = jnp.sum(pool[...] * dreward, axis=0, keepdims=True)
    scale = inv * dscore
    pull = inv * inv * inv * dscore * heads / width

    def make_dproj(j, carry):
        rows = rows_of(j)
        dp[rows, :] = (scale * both[rows, :] - z[rows, :] * pull).astype(BF16)
        return carry

    lax.fori_loop(0, per, make_dproj, 0)

    def cols_of(k):
        return exch.at[k]

    def piece(j):
        return dp.at[pl.ds(j * blk, blk)]

    def piece_copy(j):
        return pltpu.make_async_remote_copy(
            src_ref=piece(j),
            dst_ref=cols_of(me),
            send_sem=z_send.at[j],
            recv_sem=e_recv.at[me],
            device_id=replica(t * R + j),
            device_id_type=MESH,
        )

    def piece_local(j):
        return pltpu.make_async_copy(piece(j), cols_of(me), e_recv.at[me])

    for j in range(R):

        @pl.when(t * R + j != me)
        def _():
            piece_copy(j).start()

        @pl.when(t * R + j == me)
        def _():
            piece_local(j).start()

    lsrc[...] = jnp.broadcast_to(loss, lsrc.shape)
    for j in range(per):
        rows = pl.ds(j * tile, tile)
        zw = z[rows, :] * scale
        lanes = zw[:, 0:128]
        for h in range(1, tok // 128):
            lanes = lanes + zw[:, h * 128 : (h + 1) * 128]
        qsrc[0:1, j * tile : (j + 1) * tile] = jnp.sum(lanes.T, axis=0, keepdims=True)
    for d in range(1, N):
        peer_copy(lsrc, lin, l_send, l_recv, d).start()
        peer_copy(qsrc, qin, q_send, q_recv, d).start()

    owner = me // R
    rank = flip(t, owner, bits)
    step = 1 + (p // (Z - Z // 2)) * (Z - 2)

    def child_copy(j, k):
        return pltpu.make_async_remote_copy(
            src_ref=cols_of(k),
            dst_ref=cols_of(k),
            send_sem=b_send.at[j, k],
            recv_sem=e_recv.at[k],
            device_id=tensor_peer(2**j),
            device_id_type=MESH,
        )

    def place(i):
        return (o + i) % O, (p + step * (i // O)) % Z

    def forward(i):
        outer, b = place(i)
        k = outer * Z + b
        child_copy(0, k).wait_recv()
        for j in range(bits):

            @pl.when(rank < 2**j)
            def _():
                child_copy(j, k).start()

    wide = min(512, acc.shape[1])
    strips = acc.shape[1] // wide

    def strip(c):
        return pl.ds(pl.multiple_of(c * wide, wide), wide)

    def out_strip(c):
        return pltpu.make_async_copy(acc.at[:, strip(c)], grad.at[:, strip(c)], o_sem.at[c])

    def multiply(i):
        outer, b = place(i)
        k = outer * Z + b

        @pl.when(i % O > 0)
        def _():
            arrived(outer, b).wait_recv()

        def one(c, carry):
            acc[:, strip(c)] += jnp.dot(
                exch[k], attn_all[k, :, strip(c)], preferred_element_type=F32
            )

            @pl.when(i == N - 1)
            def _():
                out_strip(c).start()

            return carry

        lax.fori_loop(0, strips, one, 0)

    def first_half(i, carry):
        forward(i)
        return carry

    def second_half(i, carry):
        forward(i)

        def both_halves(h, inner):
            multiply(i - N // 2 + h * (N // 2))
            return inner

        return lax.fori_loop(0, 2, both_halves, carry)

    own_rows.wait()
    lax.fori_loop(0, N // 2, first_half, 0)
    for s in range(2, Z - 1):
        arrival(s)
    lax.fori_loop(N // 2, N, second_half, 0)

    ltotal, qtotal = lsrc[...], qsrc[...]
    for d in range(1, N):
        peer_copy(lsrc, lin, l_send, l_recv, d).wait_recv()
        peer_copy(qsrc, qin, q_send, q_recv, d).wait_recv()
        ltotal = ltotal + lin[d]
        qtotal = qtotal + qin[d]
    ltot[...] = ltotal
    qtot[...] = qtotal
    ctot[...] = jnp.broadcast_to(count, ctot.shape)

    for s in range(Z - 1):
        for ok, copy in ((right_sends(s), right_copy), (left_sends(s), left_copy)):

            @pl.when(ok)
            def _():
                copy(s).wait_send()

    for e in range(1, O):
        for b in range(Z):
            out_copy(b, e).wait_send()
    for d in range(1, N):
        peer_copy(vsum, cin, c_send, c_recv, d).wait_send()
        peer_copy(lsrc, lin, l_send, l_recv, d).wait_send()
        peer_copy(qsrc, qin, q_send, q_recv, d).wait_send()
    for r in range(1, T):
        stat_copy(r).wait_send()
        for j in range(per):
            rs_copy(r, j).wait_send()
    for j in range(R):

        @pl.when(t * R + j != me)
        def _():
            piece_copy(j).wait_send()

    def spread_end(k, carry):
        for j in range(bits):

            @pl.when(rank < 2**j)
            def _():
                child_copy(j, k).wait_send()

        return carry

    lax.fori_loop(0, N, spread_end, 0)
    for c in range(strips):
        out_strip(c).wait()


def shards(sizes, attn, out_weight, resid, norm_gain, head, lengths, pairs, pair_valid, loss_scale):
    T, O, Z = sizes
    N = O * Z
    tok, feats = resid.shape
    width = feats * T
    blk = width // N
    heads_dev = attn.shape[1]
    tile = min(512, feats)
    per = feats // tile
    seqs_dev = lengths.shape[0]
    seq_len = tok // seqs_dev
    valid = pair_valid.astype(F32)
    gain = norm_gain.astype(F32)
    headv = head.astype(F32)
    position = jnp.arange(tok)[None, :]
    mine = jnp.arange(seqs_dev)[:, None]
    member = (position % seq_len < lengths[:, None]) & (position // seq_len == mine)
    pool = member.astype(F32) / lengths.astype(F32)[:, None]
    select = (pairs[:, 0][None, :] == mine).astype(F32) - (pairs[:, 1][None, :] == mine).astype(F32)
    vsum = jnp.broadcast_to(jnp.sum(valid), (8, 128))
    vmem = pl.BlockSpec(memory_space=pltpu.VMEM)
    anyw = pl.BlockSpec(memory_space=pl.ANY)
    sem = pltpu.SemaphoreType.DMA
    bits = bits_of(T)
    grad_out_proj, qtot, ltot, ctot = pl.pallas_call(
        functools.partial(kernel, sizes),
        out_shape=(
            jax.ShapeDtypeStruct((blk, heads_dev), F32),
            jax.ShapeDtypeStruct((1, feats), F32),
            jax.ShapeDtypeStruct((8, 128), F32),
            jax.ShapeDtypeStruct((8, 128), F32),
        ),
        in_specs=[vmem, anyw, vmem, vmem, vmem, vmem, vmem, vmem, vmem],
        out_specs=(anyw, vmem, vmem, vmem),
        scratch_shapes=[
            pltpu.VMEM((N, blk, tok), BF16),
            pltpu.VMEM((N, tok, heads_dev), BF16),
            pltpu.VMEM((blk, heads_dev), F32),
            pltpu.VMEM((SLOTS, tile, heads_dev), BF16),
            pltpu.VMEM((heads_dev, tok), BF16),
            pltpu.VMEM((T, per, tile, tok), BF16),
            pltpu.VMEM((T, per, tile, tok), BF16),
            pltpu.VMEM((feats, tok), F32),
            pltpu.VMEM((feats, tok), BF16),
            pltpu.VMEM((2, tok), F32),
            pltpu.VMEM((T, 2, tok), F32),
            pltpu.VMEM((N, 8, 128), F32),
            pltpu.VMEM((8, 128), F32),
            pltpu.VMEM((N, 8, 128), F32),
            pltpu.VMEM((1, feats), F32),
            pltpu.VMEM((N, 1, feats), F32),
            sem((SLOTS,)),
            sem((T, per)),
            sem((T, per)),
            sem((T,)),
            sem((T,)),
            sem((N,)),
            sem((N,)),
            sem((N,)),
            sem((N,)),
            sem((N,)),
            sem((N,)),
            sem,
            sem((Z,)),
            sem((Z,)),
            sem((O, Z)),
            sem((O, Z)),
            sem((N // T,)),
            sem((bits, N)),
            sem((N,)),
            sem((heads_dev // min(512, heads_dev),)),
        ],
        compiler_params=pltpu.CompilerParams(
            collective_id=0, has_side_effects=True, vmem_limit_bytes=60 * 1024 * 1024
        ),
    )(
        attn,
        out_weight,
        resid,
        (gain * headv)[:, None],
        pool,
        select,
        (-loss_scale[0] * valid)[None, :],
        valid[None, :],
        vsum,
    )
    loss = (ltot[0, 0] / ctot[0, 0]).reshape(1)
    return (loss, grad_out_proj, qtot[0] * headv, qtot[0] * gain)


def solution(mesh):
    sizes = (mesh.shape["tensor"], mesh.shape["outer"], mesh.shape["dp"])
    return jax.shard_map(
        functools.partial(shards, sizes),
        mesh=mesh,
        in_specs=(
            P(("outer", "dp"), "tensor"),
            P(None, "tensor"),
            P(("outer", "dp"), "tensor"),
            P("tensor"),
            P("tensor"),
            P(("outer", "dp")),
            P(("outer", "dp"), None),
            P(("outer", "dp")),
            P(),
        ),
        out_specs=(P(), P(("outer", "dp"), "tensor"), P("tensor"), P("tensor")),
        check_vma=False,
    )
```

profile of v0, /device:TPU:6, one launch (start us, length us, event | category | flops | bytes accessed | tf_op | source)
XLA Modules:
  0.0 189.7 jit_solution(7506323772457447806)
XLA Ops:
  0.6 0.7 convert_multiply_fusion.1
  1.3 1.3 copy.13.both
  2.7 0.7 convert_element_type.24
  3.3 1.3 convert_divide_fusion.pool
  4.7 0.8 slice_bitcast_fusion.1
  5.4 0.6 convert_subtract_fusion.select
  6.7 1.8 convert_reduce_fusion
  8.5 1.2 convert_bitcast_fusion.valid
  9.6 1.2 broadcast_in_dim.19.vsum
  10.8 0.0 copy-start
  10.8 0.0 copy-start.1
  10.9 164.8 %shard_map.120 = (f32[1024,2048]{1,0:T(8,128)}, f32[1,2048]{1,0:T(1,128)}, f32[8,128]{1,0:T(8,128)}, f32[8,128]{1,0:T(8,128)}) custom-call(bf16[256,2048]{1,0:T(8,128)(2,1)} %attn.1, bf16[8192,2048]{1,0:T(8,128)(2,1)} %weight.1, bf16[256,2048]{1,0:T(8,128)(2,1)} %resid.1, f32[2048,1]{1,0:T(8,128)} %copy.13.both, f32[4,256]{1,0:T(4,128)} %convert_divide_fusion.pool, ...), custom_call_target="tpu_custom_call" | custom-call | tf_op jit(solution)/shard_map/pallas_call | solution.py:495
  175.7 1.2 slice.14
  176.9 1.2 slice.15
  179.4 0.0 copy-done
  179.4 0.0 copy-done.1
  179.4 1.3 convert_multiply_fusion.2
  180.7 7.9 %copy.16 = f32[1024,2048]{1,0:T(8,128)} copy(f32[1024,2048]{1,0:T(8,128)} %get-tuple-element.25) | data formatting | bytes 16777216
  (1 shorter events, 0.0 us)
Async XLA Ops:
  10.8 168.6 %copy-start = (bf16[2048]{0:T(1024)(128)(2,1)S(1)}, bf16[2048]{0:T(1024)(128)(2,1)}, u32[]{:S(2)}) copy-start(bf16[2048]{0:T(1024)(128)(2,1)} %param.13) | copy-start | bytes 12292
  10.8 168.6 %copy-start.1 = (bf16[2048]{0:T(1024)(128)(2,1)S(1)}, bf16[2048]{0:T(1024)(128)(2,1)}, u32[]{:S(2)}) copy-start(bf16[2048]{0:T(1024)(128)(2,1)} %param.12) | copy-start | bytes 12292
where the time goes:
time: 190 us
  Pallas kernels  165 us (87%)
  local copies, waits for them, and re-layouts  13.6 us (7%)
  other arithmetic  7.55 us (4%)
  between operations  3.78 us (2%)
    pallas_call x1, Pallas kernels, shards(): pl.pallas_call(functools.partial(kernel, sizes), out_shape=(jax.ShapeDtyp...  165 us
    unnamed x5, local copies, waits for them, and re-layouts  7.89 us

commit v1 on v0

v1 whole, which is shorter than its diff:
```python
import functools

import jax
import jax.numpy as jnp
from jax import lax
from jax.experimental import pallas as pl
from jax.experimental.pallas import tpu as pltpu
from jax.sharding import PartitionSpec as P

MESH = pl.DeviceIdType.MESH
F32 = jnp.float32
BF16 = jnp.bfloat16
SLOTS = 3


def bits_of(count):
    return count.bit_length() - 1


def flip(index, mask, bits):
    out = 0
    for j in range(bits):
        out = out + ((index // 2**j + mask // 2**j) % 2) * 2**j
    return out


def reverse(index, bits):
    out = 0
    for j in range(bits):
        out = out + ((index // 2**j) % 2) * 2 ** (bits - 1 - j)
    return out


def kernel(
    sizes,
    attn,
    weight,
    resid,
    gain,
    headv,
    lengths,
    pairs,
    pair_valid,
    loss_scale,
    grad,
    ggain,
    ghead,
    loss_out,
    exch,
    attn_all,
    wbuf,
    attn_t,
    res_t,
    vbuf,
    part,
    got,
    keep,
    dp,
    bsrc,
    ball,
    bcol,
    hacc,
    stat,
    stat_in,
    csrc,
    cin,
    lsrc,
    lin,
    qsrc,
    qin,
    qsum,
    qall,
    wsem,
    rs_send,
    rs_recv,
    b_send,
    b_recv,
    st_send,
    st_recv,
    c_send,
    c_recv,
    l_send,
    l_recv,
    q_send,
    q_recv,
    t_send,
    t_recv,
    ag_local,
    ag_right,
    ag_left,
    ag_out,
    ag_recv,
    z_send,
    z_recv,
    e_send,
    e_recv,
):
    T, O, Z = sizes
    N = O * Z
    bits = bits_of(T)
    R = N // T
    half = T // 2
    tok, feats = resid.shape
    width = feats * T
    blk = width // N
    q = blk // T
    h = q // 2
    K = (N // 2) * h
    steps = 4 * T
    o, p, t = lax.axis_index("outer"), lax.axis_index("dp"), lax.axis_index("tensor")
    me = o * Z + p

    def replica(k):
        return (k // Z, k % Z, t)

    def rank(r):
        return (o, p, r)

    barrier = pltpu.get_barrier_semaphore()
    for r in range(1, T):
        pl.semaphore_signal(barrier, inc=1, device_id=rank(flip(t, r, bits)), device_id_type=MESH)
    for d in range(1, N):
        pl.semaphore_signal(barrier, inc=1, device_id=replica((me + d) % N), device_id_type=MESH)

    def piece_of(i):
        e, g = i // 2, i % 2
        s = e % 2
        j = T - 1 - e // 2
        return s, j, g

    def target(s, j):
        return flip(t, s * j + (1 - s) * reverse(j, bits), bits)

    def load(i):
        s, j, g = piece_of(i)
        return pltpu.make_async_copy(
            weight.at[pl.ds(g * (N // 2), N // 2), target(s, j) * 2 + s],
            wbuf.at[i % SLOTS],
            wsem.at[i % SLOTS],
        )

    for i in range(min(SLOTS - 1, steps)):
        load(i).start()

    both = gain[...] * headv[...]
    for r in range(T):
        for s in range(2):
            for b in range(R):
                start = b * blk + r * q + s * h
                bsrc[r * 2 + s, 0:1, b * h : (b + 1) * h] = both[:, start : start + h]
    ball[t] = bsrc[...]
    valid = pair_valid[...].astype(F32)
    csrc[...] = jnp.broadcast_to(jnp.sum(valid, axis=1, keepdims=True), csrc.shape)

    def turn_attn(c, carry):
        cols = pl.ds(pl.multiple_of(c * 128, 128), 128)
        attn_t[cols, :] = attn[:, cols].astype(F32).T.astype(BF16)
        return carry

    lax.fori_loop(0, attn.shape[1] // 128, turn_attn, 0)
    pl.semaphore_wait(barrier, T - 1 + N - 1)

    def peer_copy(src, dst, send, recv, d):
        return pltpu.make_async_remote_copy(
            src_ref=src,
            dst_ref=dst.at[d],
            send_sem=send.at[d],
            recv_sem=recv.at[d],
            device_id=replica((me + d) % N),
            device_id_type=MESH,
        )

    def rank_copy(src, dst, send, recv, r):
        return pltpu.make_async_remote_copy(
            src_ref=src,
            dst_ref=dst,
            send_sem=send.at[r],
            recv_sem=recv.at[r],
            device_id=rank(flip(t, r, bits)),
            device_id_type=MESH,
        )

    def both_copy(r):
        return rank_copy(bsrc, ball.at[t], b_send, b_recv, r)

    for r in range(1, T):
        both_copy(r).start()

    def block_rows(outer, b):
        return outer * Z + b

    def ag_copy(src, b, send, where):
        return pltpu.make_async_remote_copy(
            src_ref=src,
            dst_ref=attn_all.at[block_rows(o, b)],
            send_sem=send,
            recv_sem=ag_recv.at[o, b],
            device_id=where,
            device_id_type=MESH,
        )

    def right_copy(s):
        b = (p + Z - s) % Z
        src = attn if s == 0 else attn_all.at[block_rows(o, b)]
        return ag_copy(src, b, ag_right.at[s], (o, (p + 1) % Z, t))

    def left_copy(s):
        b = (p + s) % Z
        src = attn if s == 0 else attn_all.at[block_rows(o, b)]
        return ag_copy(src, b, ag_left.at[s], (o, (p + Z - 1) % Z, t))

    def right_sends(s):
        return (p >= s) & (p < Z - 1)

    def left_sends(s):
        return (p + s < Z) & (p > 0)

    def out_copy(b, e, own=False):
        src = attn if own else attn_all.at[block_rows(o, b)]
        return ag_copy(src, b, ag_out.at[e, b], ((o + e) % O, p, t))

    def arrived(outer, b):
        rows = attn_all.at[block_rows(outer, b)]
        return pltpu.make_async_remote_copy(
            src_ref=rows,
            dst_ref=rows,
            send_sem=ag_out.at[0, 0],
            recv_sem=ag_recv.at[outer, b],
            device_id=(o, (p + 1) % Z, t),
            device_id_type=MESH,
        )

    def arrival(s):
        for ok, b in ((p - 1 - s >= 0, (p + Z - 1 - s) % Z), (p + 1 + s < Z, (p + 1 + s) % Z)):

            @pl.when(ok)
            def _():
                arrived(o, b).wait_recv()
                for e in range(1, O):
                    out_copy(b, e).start()

        if s + 1 < Z - 1:
            for ok, copy in ((right_sends(s + 1), right_copy), (left_sends(s + 1), left_copy)):

                @pl.when(ok)
                def _():
                    copy(s + 1).start()

    for ok, copy in ((right_sends(0), right_copy), (left_sends(0), left_copy)):

        @pl.when(ok)
        def _():
            copy(0).start()

    for e in range(1, O):
        out_copy(p, e, True).start()
    own_rows = pltpu.make_async_copy(attn, attn_all.at[block_rows(o, p)], ag_local)
    own_rows.start()
    for d in range(1, N):
        peer_copy(csrc, cin, c_send, c_recv, d).start()

    def turn_resid(c, carry):
        cols = pl.ds(pl.multiple_of(c * 128, 128), 128)
        res_t[cols, :] = resid[:, cols].astype(F32).T.astype(BF16)
        return carry

    lax.fori_loop(0, feats // 128, turn_resid, 0)
    hacc[...] = jnp.zeros_like(hacc)
    for r in range(1, T):
        both_copy(r).wait_recv()

    def rs_copy(s, j, g, mask):
        return pltpu.make_async_remote_copy(
            src_ref=part.at[s, j, g],
            dst_ref=got.at[s, j, g],
            send_sem=rs_send.at[s, j, g],
            recv_sem=rs_recv.at[s, j, g],
            device_id=rank(flip(t, mask, bits)),
            device_id_type=MESH,
        )

    def rs_mask(s, b):
        return s * 2**b + (1 - s) * 2 ** (bits - 1 - b)

    row16 = lax.broadcasted_iota(jnp.int32, (16, R * h), 0)

    def thirds(row):
        first = row.astype(BF16).astype(F32)
        second = (row - first).astype(BF16).astype(F32)
        third = row - first - second
        rows = jnp.where(row16 == 0, first, jnp.where(row16 == 1, second, third))
        return jnp.where(row16 < 3, rows, 0.0).astype(BF16)

    def project(i, carry):
        @pl.when(i + SLOTS - 1 < steps)
        def _():
            load(i + SLOTS - 1).start()

        load(i).wait()
        s, j, g = piece_of(i)
        r = target(s, j)
        vbuf[...] = jnp.dot(
            wbuf[i % SLOTS].reshape(K, wbuf.shape[3]), attn_t[...], preferred_element_type=F32
        )

        @pl.when(t // half == g)
        def _():
            for b in range(R):
                rows = pl.ds(pl.multiple_of(((t % half) * R + b) * h, h), h)
                mine = pl.ds(pl.multiple_of(b * blk + (r * 2 + s) * h, h), h)
                vbuf[rows, :] = vbuf[rows, :] + res_t[mine, :].astype(F32)

        total = hacc[...]
        for n in range(half):
            lhs = thirds(ball[g * half + n, r * 2 + s])
            rows = vbuf[n * R * h : (n + 1) * R * h, :]
            high = rows.astype(BF16)
            low = (rows - high.astype(F32)).astype(BF16)
            total = total + jnp.dot(lhs, high, preferred_element_type=F32)
            total = total + jnp.dot(lhs, low, preferred_element_type=F32)
        hacc[...] = total

        @pl.when(j >= half)
        def _():
            part[s, j, g] = vbuf[...].astype(BF16)
            rs_copy(s, j, g, rs_mask(s, bits - 1)).start()

        @pl.when(j < half)
        def _():
            keep[s, j % half, g] = vbuf[...]

        return carry

    lax.fori_loop(0, steps, project, 0)

    for b in range(bits - 2, -1, -1):

        def combine(x, carry, b=b):
            j, s, g = 2**b + x // 4, x % 2, (x // 2) % 2
            total = keep[s, j, g]
            for up in range(b + 1, bits):
                rs_copy(s, j + 2**up, g, rs_mask(s, up)).wait_recv()
                total = total + got[s, j + 2**up, g].astype(F32)
            part[s, j, g] = total.astype(BF16)
            rs_copy(s, j, g, rs_mask(s, b)).start()
            return carry

        lax.fori_loop(0, 4 * 2**b, combine, 0)

    arrival(0)

    def clear(j, carry):
        grad[pl.ds(pl.multiple_of(j * 128, 128), 128), :] = jnp.zeros((128, grad.shape[1]), F32)
        return carry

    lax.fori_loop(0, blk // 128, clear, 0)
    span = R * h
    diag = lax.broadcasted_iota(jnp.int32, (span, span), 0) == lax.broadcasted_iota(
        jnp.int32, (span, span), 1
    )

    def columns(x, carry):
        s, n = x % 2, x // 2
        row = jnp.broadcast_to(ball[n, t * 2 + s], (span, span))
        col = jnp.sum(jnp.where(diag, row, 0.0), axis=1, keepdims=True)
        rows = pl.ds(pl.multiple_of((n % half) * span, span), span)
        bcol[s, n // half, rows, :] = jnp.broadcast_to(col, (span, 128))
        return carry

    lax.fori_loop(0, 2 * T, columns, 0)

    S = lengths.shape[1]
    lens = lengths[...].astype(F32)
    same = lax.broadcasted_iota(jnp.int32, (S, S), 0) == lax.broadcasted_iota(jnp.int32, (S, S), 1)
    lens = jnp.sum(jnp.where(same, jnp.broadcast_to(lens, (S, S)), 0.0), axis=1, keepdims=True)
    seq_len = tok // S
    slot = lax.broadcasted_iota(jnp.int32, (S, tok), 1) - seq_len * lax.broadcasted_iota(
        jnp.int32, (S, tok), 0
    )
    live = (slot >= 0) & (slot.astype(F32) < lens)
    pool = jnp.where(live, 1.0 / lens, 0.0)
    who = lax.broadcasted_iota(jnp.int32, (S, pairs.shape[1]), 0)
    select = jnp.where(who == pairs[0:1, :], 1.0, 0.0) - jnp.where(who == pairs[1:2, :], 1.0, 0.0)

    def final(x, squares):
        s, g = x % 2, x // 2
        total = keep[s, 0, g]
        for up in range(bits - 1, -1, -1):
            rs_copy(s, 2**up, g, rs_mask(s, up)).wait_recv()
            total = total + got[s, 2**up, g].astype(F32)
        keep[s, 0, g] = total
        return squares + jnp.sum(total * total, axis=0, keepdims=True)

    squares = lax.fori_loop(0, 4, final, jnp.zeros((1, tok), F32))
    heads = jnp.sum(hacc[...], axis=0, keepdims=True)
    stat[0:1, :] = squares
    stat[1:2, :] = heads

    def stat_copy(r):
        return rank_copy(stat, stat_in.at[r], st_send, st_recv, r)

    for r in range(1, T):
        stat_copy(r).start()
    count = csrc[0:1, 0:1]
    for d in range(1, N):
        peer_copy(csrc, cin, c_send, c_recv, d).wait_recv()
        count = count + cin[d, 0:1, 0:1]
    for r in range(1, T):
        stat_copy(r).wait_recv()
        squares = squares + stat_in[r, 0:1, :]
        heads = heads + stat_in[r, 1:2, :]
    inv = 1.0 / jnp.sqrt(squares / width + 1e-05)
    score = heads * inv
    reward = jnp.sum(pool * score, axis=1, keepdims=True)
    margin = jnp.sum(select * reward, axis=0, keepdims=True)
    soft = jnp.maximum(-margin, 0.0) + jnp.log1p(jnp.exp(-jnp.abs(margin)))
    loss = jnp.sum(valid * soft, axis=1, keepdims=True)
    dmargin = -loss_scale[...] * valid * jax.nn.sigmoid(-margin) / count
    dreward = jnp.sum(select * dmargin, axis=1, keepdims=True)
    dscore = jnp.sum(pool * dreward, axis=0, keepdims=True)
    scale = inv * dscore
    pull = inv * inv * inv * dscore * heads / width

    def make_dproj(x, carry):
        s, g, n = x % 2, x // N, (x // 2) % (N // 2)
        rows = pl.ds(pl.multiple_of(n * h, h), h)
        spot = pl.ds(pl.multiple_of(s * h, h), h)
        for c in range(tok // 128):
            cols = slice(c * 128, (c + 1) * 128)
            dp[g * (N // 2) + n, spot, cols] = (
                scale[:, cols] * bcol[s, g, rows, :] - keep[s, 0, g, rows, cols] * pull[:, cols]
            ).astype(BF16)
        return carry

    lax.fori_loop(0, 2 * N, make_dproj, 0)

    side = p // (Z - Z // 2)
    edge = side * (Z - 1 - p) + (1 - side) * p

    def place(i):
        n = i // O
        past = (n + Z - 1 - edge) // Z
        spot = past * n + (1 - past) * (edge - n)
        return ((o + i) % O) * Z + side * (Z - 1 - spot) + (1 - side) * spot

    def slot_rows(r):
        return pl.ds(pl.multiple_of(r * q, q), q)

    def piece_copy(k):
        return pltpu.make_async_remote_copy(
            src_ref=dp.at[k],
            dst_ref=exch.at[me, slot_rows(t)],
            send_sem=z_send.at[k],
            recv_sem=z_recv.at[me],
            device_id=replica(k),
            device_id_type=MESH,
        )

    def piece_arrived(k):
        rows = exch.at[k, slot_rows(t)]
        return pltpu.make_async_remote_copy(
            src_ref=rows,
            dst_ref=rows,
            send_sem=z_send.at[k],
            recv_sem=z_recv.at[k],
            device_id=replica((me + 1) % N),
            device_id_type=MESH,
        )

    own_piece = pltpu.make_async_copy(dp.at[me], exch.at[me, slot_rows(t)], z_recv.at[me])
    own_piece.start()

    def send_piece(i, carry):
        piece_copy(place(i)).start()
        return carry

    lax.fori_loop(1, N, send_piece, 0)

    lsrc[...] = jnp.broadcast_to(loss, lsrc.shape)
    for s in range(2):
        for g in range(2):
            zw = keep[s, 0, g] * scale
            lanes = zw[:, 0:128]
            for c in range(1, tok // 128):
                lanes = lanes + zw[:, c * 128 : (c + 1) * 128]
            qsrc[s * 2 + g] = jnp.sum(lanes.T, axis=0, keepdims=True)
    for d in range(1, N):
        peer_copy(lsrc, lin, l_send, l_recv, d).start()
        peer_copy(qsrc, qin, q_send, q_recv, d).start()

    def ag_mask(s, b):
        return 2**b if s == 0 else 2 ** (bits - 1 - b)

    def held(s, c):
        return flip(t, c if s == 0 else reverse(c, bits), bits)

    def half_rows(r, s):
        return pl.ds(pl.multiple_of((r * 2 + s) * h, h), h)

    def spread_copy(k, s, c, b):
        rows = exch.at[k, half_rows(held(s, c), s)]
        return pltpu.make_async_remote_copy(
            src_ref=rows,
            dst_ref=rows,
            send_sem=e_send.at[k, s, c + 2**b],
            recv_sem=e_recv.at[k, s, c + 2**b],
            device_id=rank(flip(t, ag_mask(s, b), bits)),
            device_id_type=MESH,
        )

    def spread_arrived(k, s, c):
        rows = exch.at[k, half_rows(held(s, c), s)]
        return pltpu.make_async_remote_copy(
            src_ref=rows,
            dst_ref=rows,
            send_sem=e_send.at[k, s, c],
            recv_sem=e_recv.at[k, s, c],
            device_id=rank(flip(t, 1, bits)),
            device_id_type=MESH,
        )

    def begin(i):
        k = place(i)

        @pl.when(k == me)
        def _():
            own_piece.wait()

        @pl.when(k != me)
        def _():
            piece_arrived(k).wait_recv()

        for b in range(bits):
            for s in range(2):
                spread_copy(k, s, 0, b).start()

    def relay(i):
        k = place(i)
        for b in range(bits - 1):
            for c in range(2**b, 2 ** (b + 1)):
                for s in range(2):
                    spread_arrived(k, s, c).wait_recv()
                    for up in range(b + 1, bits):
                        spread_copy(k, s, c, up).start()

    wide = min(512, grad.shape[1])
    strips = grad.shape[1] // wide

    def multiply(i):
        k = place(i)
        outer, b = k // Z, k % Z
        for c in range(half, T):
            for s in range(2):
                spread_arrived(k, s, c).wait_recv()

        @pl.when(outer != o)
        def _():
            arrived(outer, b).wait_recv()

        def one(c, carry):
            cols = pl.ds(pl.multiple_of(c * wide, wide), wide)
            grad[:, cols] += jnp.dot(exch[k], attn_all[k, :, cols], preferred_element_type=F32)
            return carry

        lax.fori_loop(0, strips, one, 0)

    def gather_q():
        total = qsrc[...]
        for d in range(1, N):
            peer_copy(qsrc, qin, q_send, q_recv, d).wait_recv()
            total = total + qin[d]
        qsum[...] = total
        qall[t] = total
        for r in range(1, T):
            rank_copy(qsum, qall.at[t], t_send, t_recv, r).start()

    def finish_q():
        ltotal = lsrc[...]
        for d in range(1, N):
            peer_copy(lsrc, lin, l_send, l_recv, d).wait_recv()
            ltotal = ltotal + lin[d]
        loss_out[...] = ltotal[0:1, 0:1] / count
        for r in range(1, T):
            rank_copy(qsum, qall.at[t], t_send, t_recv, r).wait_recv()
        for r in range(T):
            for s in range(2):
                for b in range(R):
                    value = jnp.zeros((1, h), F32)
                    for owner in range(T):
                        n = (owner % half) * R + b
                        row = qall[r, s * 2 + owner // half]
                        value = jnp.where(t == owner, row[:, n * h : (n + 1) * h], value)
                    cols = slice(b * blk + r * q + s * h, b * blk + r * q + (s + 1) * h)
                    ggain[:, cols] = value * headv[:, cols]
                    ghead[:, cols] = value * gain[:, cols]

    own_rows.wait()

    def stage(i, carry):
        @pl.when(i < N)
        def _():
            begin(i)

        @pl.when((i >= 1) & (i < N + 1))
        def _():
            relay(i - 1)

        for s in range(1, Z - 1):

            @pl.when(i == min(2 + (s - 1) * O, N))
            def _():
                arrival(s)

        @pl.when(i == N // 2 + 1)
        def _():
            gather_q()

        @pl.when(i == N)
        def _():
            finish_q()

        @pl.when(i >= 2)
        def _():
            multiply(i - 2)

        return carry

    lax.fori_loop(0, N + 2, stage, 0)

    for s in range(Z - 1):
        for ok, copy in ((right_sends(s), right_copy), (left_sends(s), left_copy)):

            @pl.when(ok)
            def _():
                copy(s).wait_send()

    for e in range(1, O):
        for b in range(Z):
            out_copy(b, e).wait_send()
    for d in range(1, N):
        peer_copy(csrc, cin, c_send, c_recv, d).wait_send()
        peer_copy(lsrc, lin, l_send, l_recv, d).wait_send()
        peer_copy(qsrc, qin, q_send, q_recv, d).wait_send()
    for r in range(1, T):
        both_copy(r).wait_send()
        stat_copy(r).wait_send()
        rank_copy(qsum, qall.at[t], t_send, t_recv, r).wait_send()

    def rs_end(x, carry):
        s, g, j = x % 2, (x // 2) % 2, 1 + x // 4
        rs_copy(s, j, g, 1).wait_send()
        return carry

    lax.fori_loop(0, 4 * (T - 1), rs_end, 0)

    def send_end(i, carry):
        piece_copy(place(i)).wait_send()
        return carry

    lax.fori_loop(1, N, send_end, 0)

    def spread_end(k, carry):
        for b in range(bits):
            for c in range(2**b):
                for s in range(2):
                    spread_copy(k, s, c, b).wait_send()
        return carry

    lax.fori_loop(0, N, spread_end, 0)


def shards(sizes, attn, out_weight, resid, norm_gain, head, lengths, pairs, pair_valid, loss_scale):
    T, O, Z = sizes
    N = O * Z
    tok, feats = resid.shape
    width = feats * T
    blk = width // N
    q = blk // T
    h = q // 2
    K = (N // 2) * h
    R = N // T
    heads_dev = attn.shape[1]
    vmem = pl.BlockSpec(memory_space=pltpu.VMEM)
    anyw = pl.BlockSpec(memory_space=pl.ANY)
    sem = pltpu.SemaphoreType.DMA
    bits = bits_of(T)
    grad_out_proj, grad_gain, grad_head, loss = pl.pallas_call(
        functools.partial(kernel, sizes),
        out_shape=(
            pltpu.VMEM((blk, heads_dev), F32),
            jax.ShapeDtypeStruct((1, feats), F32),
            jax.ShapeDtypeStruct((1, feats), F32),
            jax.ShapeDtypeStruct((1, 1), F32),
        ),
        in_specs=[vmem, anyw] + [vmem] * 7,
        out_specs=(vmem, vmem, vmem, vmem),
        scratch_shapes=[
            pltpu.VMEM((N, blk, tok), BF16),
            pltpu.VMEM((N, tok, heads_dev), BF16),
            pltpu.VMEM((SLOTS, N // 2, h, heads_dev), BF16),
            pltpu.VMEM((heads_dev, tok), BF16),
            pltpu.VMEM((feats, tok), BF16),
            pltpu.VMEM((K, tok), F32),
            pltpu.VMEM((2, T, 2, K, tok), BF16),
            pltpu.VMEM((2, T, 2, K, tok), BF16),
            pltpu.VMEM((2, T // 2, 2, K, tok), F32),
            pltpu.VMEM((N, q, tok), BF16),
            pltpu.VMEM((2 * T, 1, R * h), F32),
            pltpu.VMEM((T, 2 * T, 1, R * h), F32),
            pltpu.VMEM((2, 2, K, 128), F32),
            pltpu.VMEM((16, tok), F32),
            pltpu.VMEM((2, tok), F32),
            pltpu.VMEM((T, 2, tok), F32),
            pltpu.VMEM((8, 128), F32),
            pltpu.VMEM((N, 8, 128), F32),
            pltpu.VMEM((8, 128), F32),
            pltpu.VMEM((N, 8, 128), F32),
            pltpu.VMEM((4, 1, K), F32),
            pltpu.VMEM((N, 4, 1, K), F32),
            pltpu.VMEM((4, 1, K), F32),
            pltpu.VMEM((T, 4, 1, K), F32),
            sem((SLOTS,)),
            sem((2, T, 2)),
            sem((2, T, 2)),
            sem((T,)),
            sem((T,)),
            sem((T,)),
            sem((T,)),
            sem((N,)),
            sem((N,)),
            sem((N,)),
            sem((N,)),
            sem((N,)),
            sem((N,)),
            sem((T,)),
            sem((T,)),
            sem,
            sem((Z,)),
            sem((Z,)),
            sem((O, Z)),
            sem((O, Z)),
            sem((N,)),
            sem((N,)),
            sem((N, 2, T)),
            sem((N, 2, T)),
        ],
        compiler_params=pltpu.CompilerParams(
            collective_id=0, has_side_effects=True, vmem_limit_bytes=50 * 1024 * 1024
        ),
    )(
        attn,
        out_weight.reshape(N, 2 * T, h, heads_dev),
        resid,
        norm_gain.astype(F32)[None, :],
        head.astype(F32)[None, :],
        lengths[None, :],
        pairs.T,
        pair_valid[None, :],
        loss_scale[None, :],
    )
    return (loss.reshape(1), grad_out_proj, grad_gain[0], grad_head[0])


def solution(mesh):
    sizes = (mesh.shape["tensor"], mesh.shape["outer"], mesh.shape["dp"])
    return jax.shard_map(
        functools.partial(shards, sizes),
        mesh=mesh,
        in_specs=(
            P(("outer", "dp"), "tensor"),
            P(None, "tensor"),
            P(("outer", "dp"), "tensor"),
            P("tensor"),
            P("tensor"),
            P(("outer", "dp")),
            P(("outer", "dp"), None),
            P(("outer", "dp")),
            P(),
        ),
        out_specs=(P(), P(("outer", "dp"), "tensor"), P("tensor"), P("tensor")),
        check_vma=False,
    )
```

time: 190 us -> 131 us (0.69)
  the two profiles are of different devices: /device:TPU:6 before, /device:TPU:0 now
where the time goes in v1:
time: 131 us
  Pallas kernels  120 us (92%)
  local copies, waits for them, and re-layouts  4.61 us (4%)
  between operations  3.06 us (2%)
  other arithmetic  2.57 us (2%)
    pallas_call x1, Pallas kernels, shards(): pl.pallas_call(functools.partial(kernel, sizes), out_shape=(pltpu.VMEM((b...  120 us
    unnamed x7, local copies, waits for them, and re-layouts  4.61 us

profile of v1, /device:TPU:0, one launch (start us, length us, event | category | flops | bytes accessed | tf_op | source)
XLA Modules:
  0.0 130.7 jit_solution(6906700785355335337)
XLA Ops:
  1.3 1.3 broadcast_in_dim.26
  2.6 1.3 broadcast_in_dim.27
  3.9 120.4 %shard_map.120 = (f32[1024,2048]{1,0:T(8,128)S(1)}, f32[1,2048]{1,0:T(1,128)}, f32[1,2048]{1,0:T(1,128)}, f32[1,1]{1,0:T(1,128)}) custom-call(bf16[256,2048]{1,0:T(8,128)(2,1)} %attn.1, bf16[8,8,128,2048]{3,2,1,0:T(8,128)(2,1)} %bitcast.11, bf16[256,2048]{1,0:T(8,128)(2,1)} %resid.1, f32[1,2048]{1,0:T(1,128)} %bitcast.12, f32[1,2048]{1,0:T(1,128)} %bitcast.13, ...), custom_call_target="tpu_custom_call" | custom-call | tf_op jit(solution)/shard_map/pallas_call | solution.py:687
  124.3 0.0 copy-start.1
  124.3 0.0 copy-start
  124.3 3.4 %copy.17 = f32[1024,2048]{1,0:T(8,128)} copy(f32[1024,2048]{1,0:T(8,128)S(1)} %get-tuple-element.13) | data formatting | bytes 16777216
  128.3 0.0 copy-done.1
  128.3 0.6 copy.20
  128.9 0.0 copy-done
  128.9 0.6 copy.21
Async XLA Ops:
  124.3 4.0 %copy-start.1 = (f32[1,2048]{1,0:T(1,128)S(1)}, f32[1,2048]{1,0:T(1,128)}, u32[]{:S(2)}) copy-start(f32[1,2048]{1,0:T(1,128)} %get-tuple-element.10) | copy-start | bytes 24580
  124.3 4.6 %copy-start = (f32[1,2048]{1,0:T(1,128)S(1)}, f32[1,2048]{1,0:T(1,128)}, u32[]{:S(2)}) copy-start(f32[1,2048]{1,0:T(1,128)} %get-tuple-element.11) | copy-start | bytes 24580

commit v2 on v1

--- a/solution.py
+++ b/solution.py
@@ -10,7 +10,7 @@
 MESH = pl.DeviceIdType.MESH
 F32 = jnp.float32
 BF16 = jnp.bfloat16
-SLOTS = 3
+SLOTS = 5
 
 
 def bits_of(count):
@@ -36,8 +36,8 @@
     attn,
     weight,
     resid,
-    gain,
-    headv,
+    gain_in,
+    head_in,
     lengths,
     pairs,
     pair_valid,
@@ -50,7 +50,10 @@
     attn_all,
     wbuf,
     attn_t,
+    res_v,
     res_t,
+    gain,
+    headv,
     vbuf,
     part,
     got,
@@ -86,6 +89,7 @@
     t_send,
     t_recv,
     ag_local,
+    r_local,
     ag_right,
     ag_left,
     ag_out,
@@ -107,6 +111,7 @@
     h = q // 2
     K = (N // 2) * h
     steps = 4 * T
+    strips, wide = attn_all.shape[1], attn_all.shape[3]
     o, p, t = lax.axis_index("outer"), lax.axis_index("dp"), lax.axis_index("tensor")
     me = o * Z + p
 
@@ -139,9 +144,24 @@
             wsem.at[i % SLOTS],
         )
 
-    for i in range(min(SLOTS - 1, steps)):
+    def strip(c):
+        return pl.ds(pl.multiple_of(c * wide, wide), wide)
+
+    def own_copy(c):
+        return pltpu.make_async_copy(attn.at[:, strip(c)], attn_all.at[me, c], ag_local.at[c])
+
+    resid_copy = pltpu.make_async_copy(resid, res_v, r_local)
+    for c in range(strips):
+        own_copy(c).start()
+    load(0).start()
+    resid_copy.start()
+    for i in range(1, min(SLOTS - 1, steps)):
         load(i).start()
 
+    lanes = gain_in.shape[1]
+    for c in range(feats // lanes):
+        gain[:, c * lanes : (c + 1) * lanes] = gain_in[c : c + 1, :].astype(F32)
+        headv[:, c * lanes : (c + 1) * lanes] = head_in[c : c + 1, :].astype(F32)
     both = gain[...] * headv[...]
     for r in range(T):
         for s in range(2):
@@ -152,12 +172,8 @@
     valid = pair_valid[...].astype(F32)
     csrc[...] = jnp.broadcast_to(jnp.sum(valid, axis=1, keepdims=True), csrc.shape)
 
-    def turn_attn(c, carry):
-        cols = pl.ds(pl.multiple_of(c * 128, 128), 128)
-        attn_t[cols, :] = attn[:, cols].astype(F32).T.astype(BF16)
-        return carry
-
-    lax.fori_loop(0, attn.shape[1] // 128, turn_attn, 0)
+    for c in range(strips):
+        own_copy(c).wait()
     pl.semaphore_wait(barrier, T - 1 + N - 1)
 
     def peer_copy(src, dst, send, recv, d):
@@ -183,31 +199,24 @@
     def both_copy(r):
         return rank_copy(bsrc, ball.at[t], b_send, b_recv, r)
 
-    for r in range(1, T):
-        both_copy(r).start()
-
     def block_rows(outer, b):
         return outer * Z + b
 
-    def ag_copy(src, b, send, where):
+    def ag_copy(b, c, send, where):
         return pltpu.make_async_remote_copy(
-            src_ref=src,
-            dst_ref=attn_all.at[block_rows(o, b)],
+            src_ref=attn_all.at[block_rows(o, b), c],
+            dst_ref=attn_all.at[block_rows(o, b), c],
             send_sem=send,
-            recv_sem=ag_recv.at[o, b],
+            recv_sem=ag_recv.at[o, b, c],
             device_id=where,
             device_id_type=MESH,
         )
 
-    def right_copy(s):
-        b = (p + Z - s) % Z
-        src = attn if s == 0 else attn_all.at[block_rows(o, b)]
-        return ag_copy(src, b, ag_right.at[s], (o, (p + 1) % Z, t))
-
-    def left_copy(s):
-        b = (p + s) % Z
-        src = attn if s == 0 else attn_all.at[block_rows(o, b)]
-        return ag_copy(src, b, ag_left.at[s], (o, (p + Z - 1) % Z, t))
+    def right_copy(s, c):
+        return ag_copy((p + Z - s) % Z, c, ag_right.at[s, c], (o, (p + 1) % Z, t))
+
+    def left_copy(s, c):
+        return ag_copy((p + s) % Z, c, ag_left.at[s, c], (o, (p + Z - 1) % Z, t))
 
     def right_sends(s):
         return (p >= s) & (p < Z - 1)
@@ -215,59 +224,75 @@
     def left_sends(s):
         return (p + s < Z) & (p > 0)
 
-    def out_copy(b, e, own=False):
-        src = attn if own else attn_all.at[block_rows(o, b)]
-        return ag_copy(src, b, ag_out.at[e, b], ((o + e) % O, p, t))
-
-    def arrived(outer, b):
-        rows = attn_all.at[block_rows(outer, b)]
+    def out_copy(b, e, c):
+        return ag_copy(b, c, ag_out.at[e, b, c], ((o + e) % O, p, t))
+
+    def arrived(outer, b, c):
+        rows = attn_all.at[block_rows(outer, b), c]
         return pltpu.make_async_remote_copy(
             src_ref=rows,
             dst_ref=rows,
-            send_sem=ag_out.at[0, 0],
-            recv_sem=ag_recv.at[outer, b],
+            send_sem=ag_out.at[0, 0, c],
+            recv_sem=ag_recv.at[outer, b, c],
             device_id=(o, (p + 1) % Z, t),
             device_id_type=MESH,
         )
 
-    def arrival(s):
+    def arrival(s, c):
         for ok, b in ((p - 1 - s >= 0, (p + Z - 1 - s) % Z), (p + 1 + s < Z, (p + 1 + s) % Z)):
 
             @pl.when(ok)
             def _():
-                arrived(o, b).wait_recv()
+                arrived(o, b, c).wait_recv()
                 for e in range(1, O):
-                    out_copy(b, e).start()
+                    out_copy(b, e, c).start()
 
         if s + 1 < Z - 1:
             for ok, copy in ((right_sends(s + 1), right_copy), (left_sends(s + 1), left_copy)):
 
                 @pl.when(ok)
                 def _():
-                    copy(s + 1).start()
+                    copy(s + 1, c).start()
+
+    def arrivals(s):
+        def one(c, carry):
+            arrival(s, c)
+            return carry
+
+        lax.fori_loop(0, strips, one, 0)
 
     for ok, copy in ((right_sends(0), right_copy), (left_sends(0), left_copy)):
 
         @pl.when(ok)
         def _():
-            copy(0).start()
-
-    for e in range(1, O):
-        out_copy(p, e, True).start()
-    own_rows = pltpu.make_async_copy(attn, attn_all.at[block_rows(o, p)], ag_local)
-    own_rows.start()
+            for c in range(strips):
+                copy(0, c).start()
+
+    for r in range(1, T):
+        both_copy(r).start()
     for d in range(1, N):
         peer_copy(csrc, cin, c_send, c_recv, d).start()
+    for e in range(1, O):
+        for c in range(strips):
+            out_copy(p, e, c).start()
+
+    def turn_attn(x, carry):
+        rows = pl.ds(pl.multiple_of(x * 128, 128), 128)
+        per = wide // 128
+        cols = pl.ds(pl.multiple_of((x % per) * 128, 128), 128)
+        attn_t[rows, :] = attn_all[me, x // per, :, cols].astype(F32).T.astype(BF16)
+        return carry
+
+    lax.fori_loop(0, attn.shape[1] // 128, turn_attn, 0)
+    resid_copy.wait()
 
     def turn_resid(c, carry):
         cols = pl.ds(pl.multiple_of(c * 128, 128), 128)
-        res_t[cols, :] = resid[:, cols].astype(F32).T.astype(BF16)
+        res_t[cols, :] = res_v[:, cols].astype(F32).T.astype(BF16)
         return carry
 
     lax.fori_loop(0, feats // 128, turn_resid, 0)
     hacc[...] = jnp.zeros_like(hacc)
-    for r in range(1, T):
-        both_copy(r).wait_recv()
 
     def rs_copy(s, j, g, mask):
         return pltpu.make_async_remote_copy(
@@ -291,47 +316,61 @@
         rows = jnp.where(row16 == 0, first, jnp.where(row16 == 1, second, third))
         return jnp.where(row16 < 3, rows, 0.0).astype(BF16)
 
-    def project(i, carry):
-        @pl.when(i + SLOTS - 1 < steps)
-        def _():
-            load(i + SLOTS - 1).start()
-
-        load(i).wait()
+    def add_heads(i):
         s, j, g = piece_of(i)
         r = target(s, j)
-        vbuf[...] = jnp.dot(
-            wbuf[i % SLOTS].reshape(K, wbuf.shape[3]), attn_t[...], preferred_element_type=F32
-        )
-
-        @pl.when(t // half == g)
-        def _():
-            for b in range(R):
-                rows = pl.ds(pl.multiple_of(((t % half) * R + b) * h, h), h)
-                mine = pl.ds(pl.multiple_of(b * blk + (r * 2 + s) * h, h), h)
-                vbuf[rows, :] = vbuf[rows, :] + res_t[mine, :].astype(F32)
-
         total = hacc[...]
         for n in range(half):
             lhs = thirds(ball[g * half + n, r * 2 + s])
-            rows = vbuf[n * R * h : (n + 1) * R * h, :]
+            rows = vbuf[i % 2, n * R * h : (n + 1) * R * h, :]
             high = rows.astype(BF16)
             low = (rows - high.astype(F32)).astype(BF16)
             total = total + jnp.dot(lhs, high, preferred_element_type=F32)
             total = total + jnp.dot(lhs, low, preferred_element_type=F32)
         hacc[...] = total
 
+    def project(i, carry):
+        @pl.when(i + SLOTS - 1 < steps)
+        def _():
+            load(i + SLOTS - 1).start()
+
+        load(i).wait()
+        s, j, g = piece_of(i)
+        r = target(s, j)
+        now = vbuf.at[i % 2]
+        now[...] = jnp.dot(
+            wbuf[i % SLOTS].reshape(K, wbuf.shape[3]), attn_t[...], preferred_element_type=F32
+        )
+
+        @pl.when(t // half == g)
+        def _():
+            for b in range(R):
+                rows = pl.ds(pl.multiple_of(((t % half) * R + b) * h, h), h)
+                mine = pl.ds(pl.multiple_of(b * blk + (r * 2 + s) * h, h), h)
+                now[rows, :] = now[rows, :] + res_t[mine, :].astype(F32)
+
         @pl.when(j >= half)
         def _():
-            part[s, j, g] = vbuf[...].astype(BF16)
+            part[s, j, g] = now[...].astype(BF16)
             rs_copy(s, j, g, rs_mask(s, bits - 1)).start()
 
         @pl.when(j < half)
         def _():
-            keep[s, j % half, g] = vbuf[...]
+            keep[s, j % half, g] = now[...]
+
+        @pl.when(i == 1)
+        def _():
+            for r in range(1, T):
+                both_copy(r).wait_recv()
+
+        @pl.when(i >= 1)
+        def _():
+            add_heads(i - 1)
 
         return carry
 
     lax.fori_loop(0, steps, project, 0)
+    add_heads(steps - 1)
 
     for b in range(bits - 2, -1, -1):
 
@@ -347,7 +386,7 @@
 
         lax.fori_loop(0, 4 * 2**b, combine, 0)
 
-    arrival(0)
+    arrivals(0)
 
     def clear(j, carry):
         grad[pl.ds(pl.multiple_of(j * 128, 128), 128), :] = jnp.zeros((128, grad.shape[1]), F32)
@@ -543,26 +582,42 @@
                     for up in range(b + 1, bits):
                         spread_copy(k, s, c, up).start()
 
-    wide = min(512, grad.shape[1])
-    strips = grad.shape[1] // wide
-
-    def multiply(i):
-        k = place(i)
-        outer, b = k // Z, k % Z
+    def add_dot(k, c):
+        grad[:, strip(c)] += jnp.dot(exch[k], attn_all[k, c], preferred_element_type=F32)
+
+    def rows_ready(k):
         for c in range(half, T):
             for s in range(2):
                 spread_arrived(k, s, c).wait_recv()
 
-        @pl.when(outer != o)
-        def _():
-            arrived(outer, b).wait_recv()
+    def multiply(i):
+        k = place(i)
+        rows_ready(k)
 
         def one(c, carry):
-            cols = pl.ds(pl.multiple_of(c * wide, wide), wide)
-            grad[:, cols] += jnp.dot(exch[k], attn_all[k, :, cols], preferred_element_type=F32)
+            @pl.when(k // Z != o)
+            def _():
+                arrived(k // Z, k % Z, c).wait_recv()
+
+            add_dot(k, c)
             return carry
 
         lax.fori_loop(0, strips, one, 0)
+
+    def last_strips(c, carry):
+        @pl.when(c < strips)
+        def _():
+            arrival(Z - 2, c)
+            add_dot(place(N - O), c)
+
+        @pl.when(c > 0)
+        def _():
+            for e in range(1, O):
+                k = place(N - O + e)
+                arrived(k // Z, k % Z, c - 1).wait_recv()
+                add_dot(k, c - 1)
+
+        return carry
 
     def gather_q():
         total = qsrc[...]
@@ -594,23 +649,21 @@
                     ggain[:, cols] = value * headv[:, cols]
                     ghead[:, cols] = value * gain[:, cols]
 
-    own_rows.wait()
-
     def stage(i, carry):
         @pl.when(i < N)
         def _():
             begin(i)
 
-        @pl.when((i >= 1) & (i < N + 1))
+        for s in range(1, Z - 2):
+
+            @pl.when(i == (1 if s == 1 else 2 + (s + 1) * O))
+            def _():
+                arrivals(s)
+
+        @pl.when(i >= 1)
         def _():
             relay(i - 1)
 
-        for s in range(1, Z - 1):
-
-            @pl.when(i == min(2 + (s - 1) * O, N))
-            def _():
-                arrival(s)
-
         @pl.when(i == N // 2 + 1)
         def _():
             gather_q()
@@ -619,24 +672,29 @@
         def _():
             finish_q()
 
-        @pl.when(i >= 2)
+        @pl.when((i >= 2) & (i < N + 2 - O))
         def _():
             multiply(i - 2)
 
         return carry
 
-    lax.fori_loop(0, N + 2, stage, 0)
+    lax.fori_loop(0, N + 1, stage, 0)
+    for e in range(O):
+        rows_ready(place(N - O + e))
+    lax.fori_loop(0, strips + 1, last_strips, 0)
 
     for s in range(Z - 1):
         for ok, copy in ((right_sends(s), right_copy), (left_sends(s), left_copy)):
 
             @pl.when(ok)
             def _():
-                copy(s).wait_send()
+                for c in range(strips):
+                    copy(s, c).wait_send()
 
     for e in range(1, O):
         for b in range(Z):
-            out_copy(b, e).wait_send()
+            for c in range(strips):
+                out_copy(b, e, c).wait_send()
     for d in range(1, N):
         peer_copy(csrc, cin, c_send, c_recv, d).wait_send()
         peer_copy(lsrc, lin, l_send, l_recv, d).wait_send()
@@ -680,6 +738,7 @@
     K = (N // 2) * h
     R = N // T
     heads_dev = attn.shape[1]
+    strips = heads_dev // min(512, heads_dev)
     vmem = pl.BlockSpec(memory_space=pltpu.VMEM)
     anyw = pl.BlockSpec(memory_space=pl.ANY)
     sem = pltpu.SemaphoreType.DMA
@@ -692,15 +751,18 @@
             jax.ShapeDtypeStruct((1, feats), F32),
             jax.ShapeDtypeStruct((1, 1), F32),
         ),
-        in_specs=[vmem, anyw] + [vmem] * 7,
+        in_specs=[anyw] * 3 + [vmem] * 6,
         out_specs=(vmem, vmem, vmem, vmem),
         scratch_shapes=[
             pltpu.VMEM((N, blk, tok), BF16),
-            pltpu.VMEM((N, tok, heads_dev), BF16),
+            pltpu.VMEM((N, strips, tok, heads_dev // strips), BF16),
             pltpu.VMEM((SLOTS, N // 2, h, heads_dev), BF16),
             pltpu.VMEM((heads_dev, tok), BF16),
+            pltpu.VMEM((tok, feats), BF16),
             pltpu.VMEM((feats, tok), BF16),
-            pltpu.VMEM((K, tok), F32),
+            pltpu.VMEM((1, feats), F32),
+            pltpu.VMEM((1, feats), F32),
+            pltpu.VMEM((2, K, tok), F32),
             pltpu.VMEM((2, T, 2, K, tok), BF16),
             pltpu.VMEM((2, T, 2, K, tok), BF16),
             pltpu.VMEM((2, T // 2, 2, K, tok), F32),
@@ -734,11 +796,12 @@
             sem((N,)),
             sem((T,)),
             sem((T,)),
+            sem((strips,)),
             sem,
-            sem((Z,)),
-            sem((Z,)),
-            sem((O, Z)),
-            sem((O, Z)),
+            sem((Z, strips)),
+            sem((Z, strips)),
+            sem((O, Z, strips)),
+            sem((O, Z, strips)),
             sem((N,)),
             sem((N,)),
             sem((N, 2, T)),
@@ -751,8 +814,8 @@
         attn,
         out_weight.reshape(N, 2 * T, h, heads_dev),
         resid,
-        norm_gain.astype(F32)[None, :],
-        head.astype(F32)[None, :],
+        norm_gain.reshape(feats // 128, 128),
+        head.reshape(feats // 128, 128),
         lengths[None, :],
         pairs.T,
         pair_valid[None, :],

time: 131 us -> 113 us (0.86)
  Pallas kernels: 120 us -> 105 us
  other arithmetic: 2.57 us -> 0 us
    pallas_call x1, Pallas kernels: 120 us -> 105 us  [shards(): pl.pallas_call(functools.partial(kernel, sizes), out_shape=(pltpu.VMEM((b...]
    broadcast_in_dim x2 -> x0, other arithmetic: 2.57 us -> none  [the longest x1 1.29 us: shards(): norm_gain.astype(F32)[None, :]]
where the time goes in v2:
time: 113 us
  Pallas kernels  105 us (93%)
  local copies, waits for them, and re-layouts  4.61 us (4%)
  between operations  3.07 us (3%)
    pallas_call x1, Pallas kernels, shards(): pl.pallas_call(functools.partial(kernel, sizes), out_shape=(pltpu.VMEM((b...  105 us
    unnamed x7, local copies, waits for them, and re-layouts  4.61 us

profile of v2, /device:TPU:0, one launch (start us, length us, event | category | flops | bytes accessed | tf_op | source)
XLA Modules:
  0.0 113.0 jit_solution(3883890617643877549)
XLA Ops:
  1.3 105.3 %shard_map.120 = (f32[1024,2048]{1,0:T(8,128)S(1)}, f32[1,2048]{1,0:T(1,128)}, f32[1,2048]{1,0:T(1,128)}, f32[1,1]{1,0:T(1,128)}) custom-call(bf16[256,2048]{1,0:T(8,128)(2,1)} %attn.1, bf16[8,8,128,2048]{3,2,1,0:T(8,128)(2,1)} %bitcast.11, bf16[256,2048]{1,0:T(8,128)(2,1)} %resid.1, bf16[16,128]{1,0:T(8,128)(2,1)} %bitcast.14, bf16[16,128]{1,0:T(8,128)(2,1)} %bitcast.15, ...), custom_call_target="tpu_custom_call" | custom-call | tf_op jit(solution)/shard_map/pallas_call | solution.py:746
  106.6 0.0 copy-start.1
  106.6 0.0 copy-start
  106.6 3.4 %copy.17 = f32[1024,2048]{1,0:T(8,128)} copy(f32[1024,2048]{1,0:T(8,128)S(1)} %get-tuple-element.13) | data formatting | bytes 16777216
  110.7 0.0 copy-done.1
  110.7 0.6 copy.20
  111.3 0.0 copy-done
  111.3 0.6 copy.21
Async XLA Ops:
  106.6 4.0 %copy-start.1 = (f32[1,2048]{1,0:T(1,128)S(1)}, f32[1,2048]{1,0:T(1,128)}, u32[]{:S(2)}) copy-start(f32[1,2048]{1,0:T(1,128)} %get-tuple-element.10) | copy-start | bytes 24580
  106.6 4.6 %copy-start = (f32[1,2048]{1,0:T(1,128)S(1)}, f32[1,2048]{1,0:T(1,128)}, u32[]{:S(2)}) copy-start(f32[1,2048]{1,0:T(1,128)} %get-tuple-element.11) | copy-start | bytes 24580

commit v3 on v2

--- a/solution.py
+++ b/solution.py
@@ -11,6 +11,7 @@
 F32 = jnp.float32
 BF16 = jnp.bfloat16
 SLOTS = 5
+PARTS = 8
 
 
 def bits_of(count):
@@ -155,8 +156,110 @@
         own_copy(c).start()
     load(0).start()
     resid_copy.start()
-    for i in range(1, min(SLOTS - 1, steps)):
-        load(i).start()
+    pl.semaphore_wait(barrier, T - 1 + N - 1)
+
+    def peer_copy(src, dst, send, recv, d):
+        return pltpu.make_async_remote_copy(
+            src_ref=src,
+            dst_ref=dst.at[d],
+            send_sem=send,
+            recv_sem=recv,
+            device_id=replica((me + d) % N),
+            device_id_type=MESH,
+        )
+
+    def rank_copy(src, dst, send, recv, r):
+        return pltpu.make_async_remote_copy(
+            src_ref=src,
+            dst_ref=dst,
+            send_sem=send,
+            recv_sem=recv,
+            device_id=rank(flip(t, r, bits)),
+            device_id_type=MESH,
+        )
+
+    def wait_all(ref, sem):
+        pltpu.make_async_copy(ref, ref, sem).wait()
+
+    def both_copy(r):
+        return rank_copy(bsrc, ball.at[t], b_send, b_recv, r)
+
+    def block_rows(outer, b):
+        return outer * Z + b
+
+    def ag_copy(b, c, send, where, own=False):
+        return pltpu.make_async_remote_copy(
+            src_ref=attn.at[:, strip(c)] if own else attn_all.at[block_rows(o, b), c],
+            dst_ref=attn_all.at[block_rows(o, b), c],
+            send_sem=send,
+            recv_sem=ag_recv.at[o, b, c],
+            device_id=where,
+            device_id_type=MESH,
+        )
+
+    def right_copy(s, c):
+        return ag_copy((p + Z - s) % Z, c, ag_right.at[s], (o, (p + 1) % Z, t), s == 0)
+
+    def left_copy(s, c):
+        return ag_copy((p + s) % Z, c, ag_left.at[s], (o, (p + Z - 1) % Z, t), s == 0)
+
+    def right_sends(s):
+        return (p >= s) & (p < Z - 1)
+
+    def left_sends(s):
+        return (p + s < Z) & (p > 0)
+
+    def out_copy(b, e, c):
+        return ag_copy(b, c, ag_out.at[e], ((o + e) % O, p, t))
+
+    def arrived(outer, b, c):
+        rows = attn_all.at[block_rows(outer, b), c]
+        return pltpu.make_async_remote_copy(
+            src_ref=rows,
+            dst_ref=rows,
+            send_sem=ag_out.at[0],
+            recv_sem=ag_recv.at[outer, b, c],
+            device_id=(o, (p + 1) % Z, t),
+            device_id_type=MESH,
+        )
+
+    def arrival(s, c, ends=False):
+        for ok, b in ((p - 1 - s >= 0, (p + Z - 1 - s) % Z), (p + 1 + s < Z, (p + 1 + s) % Z)):
+
+            @pl.when(ok)
+            def _():
+                arrived(o, b, c).wait_recv()
+                for e in range(1, O):
+                    out_copy(b, e, c).start()
+
+        if s + 1 < Z - 1:
+            for ok, copy in relays(s + 1, ends):
+
+                @pl.when(ok)
+                def _():
+                    copy(s + 1, c).start()
+
+    def relays(s, ends=False, inner=False):
+        right, left = right_sends(s), left_sends(s)
+        if ends:
+            right, left = right & (p + 2 == Z), left & (p == 1)
+        if inner:
+            right, left = right & (p + 2 < Z), left & (p > 1)
+        return (right, right_copy), (left, left_copy)
+
+    def arrivals(s, first, last, ends=False):
+        def one(c, carry):
+            arrival(s, c, ends)
+            return carry
+
+        lax.fori_loop(first, last, one, 0)
+
+    for ok, copy in ((right_sends(0), right_copy), (left_sends(0), left_copy)):
+
+        @pl.when(ok)
+        def _():
+            for c in range(strips):
+                copy(0, c).start()
 
     lanes = gain_in.shape[1]
     for c in range(feats // lanes):
@@ -172,134 +275,44 @@
     valid = pair_valid[...].astype(F32)
     csrc[...] = jnp.broadcast_to(jnp.sum(valid, axis=1, keepdims=True), csrc.shape)
 
-    for c in range(strips):
-        own_copy(c).wait()
-    pl.semaphore_wait(barrier, T - 1 + N - 1)
-
-    def peer_copy(src, dst, send, recv, d):
-        return pltpu.make_async_remote_copy(
-            src_ref=src,
-            dst_ref=dst.at[d],
-            send_sem=send.at[d],
-            recv_sem=recv.at[d],
-            device_id=replica((me + d) % N),
-            device_id_type=MESH,
-        )
-
-    def rank_copy(src, dst, send, recv, r):
-        return pltpu.make_async_remote_copy(
-            src_ref=src,
-            dst_ref=dst,
-            send_sem=send.at[r],
-            recv_sem=recv.at[r],
-            device_id=rank(flip(t, r, bits)),
-            device_id_type=MESH,
-        )
-
-    def both_copy(r):
-        return rank_copy(bsrc, ball.at[t], b_send, b_recv, r)
-
-    def block_rows(outer, b):
-        return outer * Z + b
-
-    def ag_copy(b, c, send, where):
-        return pltpu.make_async_remote_copy(
-            src_ref=attn_all.at[block_rows(o, b), c],
-            dst_ref=attn_all.at[block_rows(o, b), c],
-            send_sem=send,
-            recv_sem=ag_recv.at[o, b, c],
-            device_id=where,
-            device_id_type=MESH,
-        )
-
-    def right_copy(s, c):
-        return ag_copy((p + Z - s) % Z, c, ag_right.at[s, c], (o, (p + 1) % Z, t))
-
-    def left_copy(s, c):
-        return ag_copy((p + s) % Z, c, ag_left.at[s, c], (o, (p + Z - 1) % Z, t))
-
-    def right_sends(s):
-        return (p >= s) & (p < Z - 1)
-
-    def left_sends(s):
-        return (p + s < Z) & (p > 0)
-
-    def out_copy(b, e, c):
-        return ag_copy(b, c, ag_out.at[e, b, c], ((o + e) % O, p, t))
-
-    def arrived(outer, b, c):
-        rows = attn_all.at[block_rows(outer, b), c]
-        return pltpu.make_async_remote_copy(
-            src_ref=rows,
-            dst_ref=rows,
-            send_sem=ag_out.at[0, 0, c],
-            recv_sem=ag_recv.at[outer, b, c],
-            device_id=(o, (p + 1) % Z, t),
-            device_id_type=MESH,
-        )
-
-    def arrival(s, c):
-        for ok, b in ((p - 1 - s >= 0, (p + Z - 1 - s) % Z), (p + 1 + s < Z, (p + 1 + s) % Z)):
-
-            @pl.when(ok)
-            def _():
-                arrived(o, b, c).wait_recv()
-                for e in range(1, O):
-                    out_copy(b, e, c).start()
-
-        if s + 1 < Z - 1:
-            for ok, copy in ((right_sends(s + 1), right_copy), (left_sends(s + 1), left_copy)):
-
-                @pl.when(ok)
-                def _():
-                    copy(s + 1, c).start()
-
-    def arrivals(s):
-        def one(c, carry):
-            arrival(s, c)
-            return carry
-
-        lax.fori_loop(0, strips, one, 0)
-
-    for ok, copy in ((right_sends(0), right_copy), (left_sends(0), left_copy)):
-
-        @pl.when(ok)
-        def _():
-            for c in range(strips):
-                copy(0, c).start()
-
     for r in range(1, T):
         both_copy(r).start()
     for d in range(1, N):
         peer_copy(csrc, cin, c_send, c_recv, d).start()
-    for e in range(1, O):
-        for c in range(strips):
+    for c in range(strips):
+        own_copy(c).wait()
+        for e in range(1, O):
             out_copy(p, e, c).start()
+    for i in range(1, min(SLOTS - 1, steps)):
+        load(i).start()
 
     def turn_attn(x, carry):
         rows = pl.ds(pl.multiple_of(x * 128, 128), 128)
         per = wide // 128
         cols = pl.ds(pl.multiple_of((x % per) * 128, 128), 128)
-        attn_t[rows, :] = attn_all[me, x // per, :, cols].astype(F32).T.astype(BF16)
+        attn_t[rows, :] = attn_all[me, x // per, :, cols].T
         return carry
 
     lax.fori_loop(0, attn.shape[1] // 128, turn_attn, 0)
     resid_copy.wait()
 
-    def turn_resid(c, carry):
-        cols = pl.ds(pl.multiple_of(c * 128, 128), 128)
-        res_t[cols, :] = res_v[:, cols].astype(F32).T.astype(BF16)
-        return carry
-
-    lax.fori_loop(0, feats // 128, turn_resid, 0)
+    if h % 128 > 0:
+
+        def turn_resid(c, carry):
+            cols = pl.ds(pl.multiple_of(c * 128, 128), 128)
+            res_t[cols, :] = res_v[:, cols].T
+            return carry
+
+        lax.fori_loop(0, feats // 128, turn_resid, 0)
+
     hacc[...] = jnp.zeros_like(hacc)
 
     def rs_copy(s, j, g, mask):
         return pltpu.make_async_remote_copy(
             src_ref=part.at[s, j, g],
             dst_ref=got.at[s, j, g],
-            send_sem=rs_send.at[s, j, g],
-            recv_sem=rs_recv.at[s, j, g],
+            send_sem=rs_send,
+            recv_sem=rs_recv.at[s, j - 1, g],
             device_id=rank(flip(t, mask, bits)),
             device_id_type=MESH,
         )
@@ -347,7 +360,11 @@
             for b in range(R):
                 rows = pl.ds(pl.multiple_of(((t % half) * R + b) * h, h), h)
                 mine = pl.ds(pl.multiple_of(b * blk + (r * 2 + s) * h, h), h)
-                now[rows, :] = now[rows, :] + res_t[mine, :].astype(F32)
+                if h % 128 > 0:
+                    extra = res_t[mine, :].astype(F32)
+                else:
+                    extra = res_v[:, mine].astype(F32).T
+                now[rows, :] = now[rows, :] + extra
 
         @pl.when(j >= half)
         def _():
@@ -360,8 +377,7 @@
 
         @pl.when(i == 1)
         def _():
-            for r in range(1, T):
-                both_copy(r).wait_recv()
+            wait_all(ball.at[pl.ds(0, T - 1)], b_recv)
 
         @pl.when(i >= 1)
         def _():
@@ -386,7 +402,9 @@
 
         lax.fori_loop(0, 4 * 2**b, combine, 0)
 
-    arrivals(0)
+    early = max(1, strips - 1)
+    arrivals(0, 0, early)
+    arrivals(0, early, strips, True)
 
     def clear(j, carry):
         grad[pl.ds(pl.multiple_of(j * 128, 128), 128), :] = jnp.zeros((128, grad.shape[1]), F32)
@@ -441,11 +459,11 @@
     for r in range(1, T):
         stat_copy(r).start()
     count = csrc[0:1, 0:1]
+    wait_all(cin.at[pl.ds(1, N - 1)], c_recv)
     for d in range(1, N):
-        peer_copy(csrc, cin, c_send, c_recv, d).wait_recv()
         count = count + cin[d, 0:1, 0:1]
+    wait_all(stat_in.at[pl.ds(1, T - 1)], st_recv)
     for r in range(1, T):
-        stat_copy(r).wait_recv()
         squares = squares + stat_in[r, 0:1, :]
         heads = heads + stat_in[r, 1:2, :]
     inv = 1.0 / jnp.sqrt(squares / width + 1e-05)
@@ -489,7 +507,7 @@
         return pltpu.make_async_remote_copy(
             src_ref=dp.at[k],
             dst_ref=exch.at[me, slot_rows(t)],
-            send_sem=z_send.at[k],
+            send_sem=z_send,
             recv_sem=z_recv.at[me],
             device_id=replica(k),
             device_id_type=MESH,
@@ -500,7 +518,7 @@
         return pltpu.make_async_remote_copy(
             src_ref=rows,
             dst_ref=rows,
-            send_sem=z_send.at[k],
+            send_sem=z_send,
             recv_sem=z_recv.at[k],
             device_id=replica((me + 1) % N),
             device_id_type=MESH,
@@ -513,7 +531,12 @@
         piece_copy(place(i)).start()
         return carry
 
-    lax.fori_loop(1, N, send_piece, 0)
+    lax.fori_loop(1, N // 2, send_piece, 0)
+
+    @pl.when(edge > 0)
+    def _():
+        lax.fori_loop(N // 2, N, send_piece, 0)
+
 
     lsrc[...] = jnp.broadcast_to(loss, lsrc.shape)
     for s in range(2):
@@ -526,6 +549,13 @@
     for d in range(1, N):
         peer_copy(lsrc, lin, l_send, l_recv, d).start()
         peer_copy(qsrc, qin, q_send, q_recv, d).start()
+    for c in range(early, strips):
+        for ok, copy in relays(1, inner=True):
+
+            @pl.when(ok)
+            def _():
+                copy(1, c).start()
+
 
     def ag_mask(s, b):
         return 2**b if s == 0 else 2 ** (bits - 1 - b)
@@ -541,22 +571,14 @@
         return pltpu.make_async_remote_copy(
             src_ref=rows,
             dst_ref=rows,
-            send_sem=e_send.at[k, s, c + 2**b],
-            recv_sem=e_recv.at[k, s, c + 2**b],
+            send_sem=e_send,
+            recv_sem=e_recv.at[k, b],
             device_id=rank(flip(t, ag_mask(s, b), bits)),
             device_id_type=MESH,
         )
 
-    def spread_arrived(k, s, c):
-        rows = exch.at[k, half_rows(held(s, c), s)]
-        return pltpu.make_async_remote_copy(
-            src_ref=rows,
-            dst_ref=rows,
-            send_sem=e_send.at[k, s, c],
-            recv_sem=e_recv.at[k, s, c],
-            device_id=rank(flip(t, 1, bits)),
-            device_id_type=MESH,
-        )
+    def spread_arrived(k, b):
+        wait_all(exch.at[k, pl.ds(0, q * 2**b)], e_recv.at[k, b])
 
     def begin(i):
         k = place(i)
@@ -576,9 +598,9 @@
     def relay(i):
         k = place(i)
         for b in range(bits - 1):
+            spread_arrived(k, b)
             for c in range(2**b, 2 ** (b + 1)):
                 for s in range(2):
-                    spread_arrived(k, s, c).wait_recv()
                     for up in range(b + 1, bits):
                         spread_copy(k, s, c, up).start()
 
@@ -586,9 +608,7 @@
         grad[:, strip(c)] += jnp.dot(exch[k], attn_all[k, c], preferred_element_type=F32)
 
     def rows_ready(k):
-        for c in range(half, T):
-            for s in range(2):
-                spread_arrived(k, s, c).wait_recv()
+        spread_arrived(k, bits - 1)
 
     def multiply(i):
         k = place(i)
@@ -621,8 +641,8 @@
 
     def gather_q():
         total = qsrc[...]
+        wait_all(qin.at[pl.ds(1, N - 1)], q_recv)
         for d in range(1, N):
-            peer_copy(qsrc, qin, q_send, q_recv, d).wait_recv()
             total = total + qin[d]
         qsum[...] = total
         qall[t] = total
@@ -631,12 +651,11 @@
 
     def finish_q():
         ltotal = lsrc[...]
+        wait_all(lin.at[pl.ds(1, N - 1)], l_recv)
         for d in range(1, N):
-            peer_copy(lsrc, lin, l_send, l_recv, d).wait_recv()
             ltotal = ltotal + lin[d]
         loss_out[...] = ltotal[0:1, 0:1] / count
-        for r in range(1, T):
-            rank_copy(qsum, qall.at[t], t_send, t_recv, r).wait_recv()
+        wait_all(qall.at[pl.ds(0, T - 1)], t_recv)
         for r in range(T):
             for s in range(2):
                 for b in range(R):
@@ -654,17 +673,27 @@
         def _():
             begin(i)
 
+        @pl.when((i == O) & (edge == 0))
+        def _():
+            lax.fori_loop(N // 2, N, send_piece, 0)
+
         for s in range(1, Z - 2):
 
-            @pl.when(i == (1 if s == 1 else 2 + (s + 1) * O))
+            @pl.when(i == (O if s == 1 else 2 + (s + 1) * O))
             def _():
-                arrivals(s)
+                arrivals(s, 0, early if s == 1 else strips)
+
+            if s == 1:
+
+                @pl.when(i == 2 + 2 * O)
+                def _():
+                    arrivals(1, early, strips)
 
         @pl.when(i >= 1)
         def _():
             relay(i - 1)
 
-        @pl.when(i == N // 2 + 1)
+        @pl.when(i == N - 2)
         def _():
             gather_q()
 
@@ -684,47 +713,37 @@
     lax.fori_loop(0, strips + 1, last_strips, 0)
 
     for s in range(Z - 1):
-        for ok, copy in ((right_sends(s), right_copy), (left_sends(s), left_copy)):
+        for ok, sem in ((right_sends(s), ag_right), (left_sends(s), ag_left)):
 
             @pl.when(ok)
             def _():
-                for c in range(strips):
-                    copy(s, c).wait_send()
+                wait_all(attn_all.at[0], sem.at[s])
 
     for e in range(1, O):
-        for b in range(Z):
-            for c in range(strips):
-                out_copy(b, e, c).wait_send()
-    for d in range(1, N):
-        peer_copy(csrc, cin, c_send, c_recv, d).wait_send()
-        peer_copy(lsrc, lin, l_send, l_recv, d).wait_send()
-        peer_copy(qsrc, qin, q_send, q_recv, d).wait_send()
-    for r in range(1, T):
-        both_copy(r).wait_send()
-        stat_copy(r).wait_send()
-        rank_copy(qsum, qall.at[t], t_send, t_recv, r).wait_send()
-
-    def rs_end(x, carry):
-        s, g, j = x % 2, (x // 2) % 2, 1 + x // 4
-        rs_copy(s, j, g, 1).wait_send()
-        return carry
-
-    lax.fori_loop(0, 4 * (T - 1), rs_end, 0)
-
-    def send_end(i, carry):
-        piece_copy(place(i)).wait_send()
-        return carry
-
-    lax.fori_loop(1, N, send_end, 0)
-
-    def spread_end(k, carry):
-        for b in range(bits):
-            for c in range(2**b):
-                for s in range(2):
-                    spread_copy(k, s, c, b).wait_send()
-        return carry
-
-    lax.fori_loop(0, N, spread_end, 0)
+        wait_all(attn_all.at[pl.ds(0, Z)], ag_out.at[e])
+    wait_all(cin.at[pl.ds(1, N - 1)], c_send)
+    wait_all(lin.at[pl.ds(1, N - 1)], l_send)
+    wait_all(qin.at[pl.ds(1, N - 1)], q_send)
+    wait_all(ball.at[pl.ds(0, T - 1)], b_send)
+    wait_all(stat_in.at[pl.ds(1, T - 1)], st_send)
+    wait_all(qall.at[pl.ds(0, T - 1)], t_send)
+    wait_all(part.at[:, pl.ds(1, T - 1)], rs_send)
+    wait_all(dp.at[pl.ds(0, N - 1)], z_send)
+    wait_all(exch.at[:, pl.ds(0, (T - 1) * q)], e_send)
+
+
+def write_out(grad, ggain, ghead, loss, grad_o, ggain_o, ghead_o, loss_o, sems):
+    rows = grad.shape[0] // PARTS
+    copies = []
+    for i in range(PARTS):
+        part = pl.ds(i * rows, rows)
+        copies.append(pltpu.make_async_copy(grad.at[part], grad_o.at[part], sems.at[i]))
+    for i, (src, dst) in enumerate(((ggain, ggain_o), (ghead, ghead_o), (loss, loss_o))):
+        copies.append(pltpu.make_async_copy(src, dst, sems.at[PARTS + i]))
+    for copy in copies:
+        copy.start()
+    for copy in copies:
+        copy.wait()
 
 
 def shards(sizes, attn, out_weight, resid, norm_gain, head, lengths, pairs, pair_valid, loss_scale):
@@ -743,13 +762,13 @@
     anyw = pl.BlockSpec(memory_space=pl.ANY)
     sem = pltpu.SemaphoreType.DMA
     bits = bits_of(T)
-    grad_out_proj, grad_gain, grad_head, loss = pl.pallas_call(
+    results = pl.pallas_call(
         functools.partial(kernel, sizes),
         out_shape=(
             pltpu.VMEM((blk, heads_dev), F32),
-            jax.ShapeDtypeStruct((1, feats), F32),
-            jax.ShapeDtypeStruct((1, feats), F32),
-            jax.ShapeDtypeStruct((1, 1), F32),
+            pltpu.VMEM((1, feats), F32),
+            pltpu.VMEM((1, feats), F32),
+            pltpu.VMEM((1, 1), F32),
         ),
         in_specs=[anyw] * 3 + [vmem] * 6,
         out_specs=(vmem, vmem, vmem, vmem),
@@ -782,30 +801,30 @@
             pltpu.VMEM((4, 1, K), F32),
             pltpu.VMEM((T, 4, 1, K), F32),
             sem((SLOTS,)),
-            sem((2, T, 2)),
-            sem((2, T, 2)),
-            sem((T,)),
-            sem((T,)),
-            sem((T,)),
-            sem((T,)),
+            sem,
+            sem((2, T - 1, 2)),
+            sem,
+            sem,
+            sem,
+            sem,
+            sem,
+            sem,
+            sem,
+            sem,
+            sem,
+            sem,
+            sem,
+            sem,
+            sem((strips,)),
+            sem,
+            sem((Z,)),
+            sem((Z,)),
+            sem((O,)),
+            sem((O, Z, strips)),
+            sem,
             sem((N,)),
-            sem((N,)),
-            sem((N,)),
-            sem((N,)),
-            sem((N,)),
-            sem((N,)),
-            sem((T,)),
-            sem((T,)),
-            sem((strips,)),
-            sem,
-            sem((Z, strips)),
-            sem((Z, strips)),
-            sem((O, Z, strips)),
-            sem((O, Z, strips)),
-            sem((N,)),
-            sem((N,)),
-            sem((N, 2, T)),
-            sem((N, 2, T)),
+            sem,
+            sem((N, bits)),
         ],
         compiler_params=pltpu.CompilerParams(
             collective_id=0, has_side_effects=True, vmem_limit_bytes=50 * 1024 * 1024
@@ -821,6 +840,19 @@
         pair_valid[None, :],
         loss_scale[None, :],
     )
+    grad_out_proj, grad_gain, grad_head, loss = pl.pallas_call(
+        write_out,
+        out_shape=(
+            jax.ShapeDtypeStruct((blk, heads_dev), F32),
+            jax.ShapeDtypeStruct((1, feats), F32),
+            jax.ShapeDtypeStruct((1, feats), F32),
+            jax.ShapeDtypeStruct((1, 1), F32),
+        ),
+        in_specs=[anyw] * 4,
+        out_specs=(anyw,) * 4,
+        scratch_shapes=[sem((PARTS + 3,))],
+        compiler_params=pltpu.CompilerParams(vmem_limit_bytes=1024 * 1024),
+    )(*results)
     return (loss.reshape(1), grad_out_proj, grad_gain[0], grad_head[0])
 
 

time: 113 us -> 104 us (0.920)
  local copies, waits for them, and re-layouts: 4.61 us -> 0 us
  Pallas kernels: 105 us -> 103 us
  between operations: 3.07 us -> 1.29 us
    pallas_call x1, Pallas kernels: 105 us -> 98.6 us  [shards(): pl.pallas_call(functools.partial(kernel, sizes), out_shape=(pltpu.VMEM((b...]
    unnamed x7 -> x0, local copies, waits for them, and re-layouts: 4.61 us -> none
    pallas_call x0 -> x1, Pallas kernels: none -> 4.03 us  [shards(): pl.pallas_call(write_out, out_shape=(jax.ShapeDtypeStruct((blk, heads_dev...]
where the time goes in v3:
time: 104 us
  Pallas kernels  103 us (99%)
  between operations  1.29 us (1%)
    pallas_call x1, Pallas kernels, shards(): pl.pallas_call(functools.partial(kernel, sizes), out_shape=(pltpu.VMEM((b...  98.6 us
    pallas_call x1, Pallas kernels, shards(): pl.pallas_call(write_out, out_shape=(jax.ShapeDtypeStruct((blk, heads_dev...  4.03 us

profile of v3, /device:TPU:0, one launch (start us, length us, event | category | flops | bytes accessed | tf_op | source)
XLA Modules:
  0.0 104.0 jit_solution(1960192783613886049)
XLA Ops:
  1.3 98.6 %shard_map.120 = (f32[1024,2048]{1,0:T(8,128)S(1)}, f32[1,2048]{1,0:T(1,128)S(1)}, f32[1,2048]{1,0:T(1,128)S(1)}, f32[1,1]{1,0:T(1,128)}) custom-call(bf16[256,2048]{1,0:T(8,128)(2,1)} %attn.1, bf16[8,8,128,2048]{3,2,1,0:T(8,128)(2,1)} %bitcast.11, bf16[256,2048]{1,0:T(8,128)(2,1)} %resid.1, bf16[16,128]{1,0:T(8,128)(2,1)} %bitcast.12, ...), custom_call_target="tpu_custom_call" | custom-call | tf_op jit(solution)/shard_map/pallas_call | solution.py:765
  99.9 4.0 %shard_map.121 = (f32[1024,2048]{1,0:T(8,128)}, f32[1,2048]{1,0:T(1,128)}, f32[1,2048]{1,0:T(1,128)}, f32[1,1]{1,0:T(1,128)}) custom-call(f32[1024,2048]{1,0:T(8,128)S(1)} %get-tuple-element.12.grad, f32[1,2048]{1,0:T(1,128)S(1)} %get-tuple-element.13.ggain, f32[1,2048]{1,0:T(1,128)S(1)} %get-tuple-element.14.ghead, f32[1,1]{1,0:T(1,128)} %get-tuple-element.15.loss), custom_call_target="tpu_custom_call" | custom-call | tf_op jit(solution)/shard_map/pallas_call | solution.py:843

commit v4 on v3

--- a/solution.py
+++ b/solution.py
@@ -30,6 +30,17 @@
     for j in range(bits):
         out = out + ((index // 2**j) % 2) * 2 ** (bits - 1 - j)
     return out
+
+
+def encode(value):
+    square = value * value
+    return (value * jnp.abs(value) * square * (square * square)).astype(BF16)
+
+
+def decode(code):
+    code = code.astype(F32)
+    size = jnp.sqrt(jnp.sqrt(jnp.sqrt(jnp.abs(code))))
+    return jnp.where(code < 0.0, -size, size)
 
 
 def kernel(
@@ -368,7 +379,7 @@
 
         @pl.when(j >= half)
         def _():
-            part[s, j, g] = now[...].astype(BF16)
+            part[s, j, g] = encode(now[...])
             rs_copy(s, j, g, rs_mask(s, bits - 1)).start()
 
         @pl.when(j < half)
@@ -395,8 +406,8 @@
             total = keep[s, j, g]
             for up in range(b + 1, bits):
                 rs_copy(s, j + 2**up, g, rs_mask(s, up)).wait_recv()
-                total = total + got[s, j + 2**up, g].astype(F32)
-            part[s, j, g] = total.astype(BF16)
+                total = total + decode(got[s, j + 2**up, g])
+            part[s, j, g] = encode(total)
             rs_copy(s, j, g, rs_mask(s, b)).start()
             return carry
 
@@ -444,7 +455,7 @@
         total = keep[s, 0, g]
         for up in range(bits - 1, -1, -1):
             rs_copy(s, 2**up, g, rs_mask(s, up)).wait_recv()
-            total = total + got[s, 2**up, g].astype(F32)
+            total = total + decode(got[s, 2**up, g])
         keep[s, 0, g] = total
         return squares + jnp.sum(total * total, axis=0, keepdims=True)
 
@@ -673,13 +684,13 @@
         def _():
             begin(i)
 
-        @pl.when((i == O) & (edge == 0))
+        @pl.when((i == O+1) & (edge == 0))
         def _():
             lax.fori_loop(N // 2, N, send_piece, 0)
 
         for s in range(1, Z - 2):
 
-            @pl.when(i == (O if s == 1 else 2 + (s + 1) * O))
+            @pl.when(i == (1 if s == 1 else 2 + (s + 1) * O))
             def _():
                 arrivals(s, 0, early if s == 1 else strips)
 

time: 104 us -> 102 us (0.981)
  Pallas kernels: 103 us -> 101 us
    pallas_call x1, Pallas kernels: 98.6 us -> 96.8 us  [shards(): pl.pallas_call(functools.partial(kernel, sizes), out_shape=(pltpu.VMEM((b...]
where the time goes in v4:
time: 102 us
  Pallas kernels  101 us (99%)
  between operations  1.29 us (1%)
    pallas_call x1, Pallas kernels, shards(): pl.pallas_call(functools.partial(kernel, sizes), out_shape=(pltpu.VMEM((b...  96.8 us
    pallas_call x1, Pallas kernels, shards(): pl.pallas_call(write_out, out_shape=(jax.ShapeDtypeStruct((blk, heads_dev...  4.03 us

profile of v4, /device:TPU:0, one launch (start us, length us, event | category | flops | bytes accessed | tf_op | source)
XLA Modules:
  0.0 102.1 jit_solution(13636684422216631359)
XLA Ops:
  1.3 96.8 %shard_map.120 = (f32[1024,2048]{1,0:T(8,128)S(1)}, f32[1,2048]{1,0:T(1,128)S(1)}, f32[1,2048]{1,0:T(1,128)S(1)}, f32[1,1]{1,0:T(1,128)}) custom-call(bf16[256,2048]{1,0:T(8,128)(2,1)} %attn.1, bf16[8,8,128,2048]{3,2,1,0:T(8,128)(2,1)} %bitcast.11, bf16[256,2048]{1,0:T(8,128)(2,1)} %resid.1, bf16[16,128]{1,0:T(8,128)(2,1)} %bitcast.12, ...), custom_call_target="tpu_custom_call" | custom-call | tf_op jit(solution)/shard_map/pallas_call | solution.py:776
  98.1 4.0 %shard_map.121 = (f32[1024,2048]{1,0:T(8,128)}, f32[1,2048]{1,0:T(1,128)}, f32[1,2048]{1,0:T(1,128)}, f32[1,1]{1,0:T(1,128)}) custom-call(f32[1024,2048]{1,0:T(8,128)S(1)} %get-tuple-element.12.grad, f32[1,2048]{1,0:T(1,128)S(1)} %get-tuple-element.13.ggain, f32[1,2048]{1,0:T(1,128)S(1)} %get-tuple-element.14.ghead, f32[1,1]{1,0:T(1,128)} %get-tuple-element.15.loss), custom_call_target="tpu_custom_call" | custom-call | tf_op jit(solution)/shard_map/pallas_call | solution.py:854
